TPU v7x, 512 devices: a whole 4x8x8 slice. The times are simulated.
512 devices in a mesh: rad: 16 (over z_hi, x, core), harm: 32 (over y, z_lo).
Axes of the slice: x: 4, y: 8, z: 8 (z_hi: 2, z_lo: 4; z = z_hi * 4 + z_lo), core: 2. Of those that a mesh axis runs over, the one named last changes fastest.
Arguments:
- velocity: bfloat16 [3, 64, 2, 256, 256], P(None, 'rad', None, 'harm'), may hold values from -6 to 6
- magnetic: bfloat16 [3, 64, 2, 256, 256], P(None, 'rad', None, 'harm'), may hold values from -6 to 6
- vorticity: bfloat16 [3, 64, 2, 256, 256], P(None, 'rad', None, 'harm'), may hold values from -6 to 6
- current: bfloat16 [3, 64, 2, 256, 256], P(None, 'rad', None, 'harm'), may hold values from -6 to 6
Outputs:
- advection: bfloat16 [3, 64, 2, 256, 256], P(None, 'rad', None, 'harm')
- induction_gradient: bfloat16 [3, 64, 2, 256, 256], P(None, 'rad', None, 'harm')
- energy_spectra: float32 [2, 64, 256], P(None, 'rad')
All inputs are finite; a program needn't handle non-finite values.
Results may differ from a plain program's by a relative error of at most 0.01.
Values may be sent and summed in bfloat16 or wider, within the bound.
A program may use at most 64 MiB of HBM per device.

v0:
```python
import jax
import jax.numpy as jnp
from jax import lax
from jax.sharding import PartitionSpec as P


def sent_to_all(shard, axis):
    count = lax.axis_size(axis)
    return lax.all_to_all(
        jnp.broadcast_to(shard[None], (count, *shard.shape)), axis, 0, 0, tiled=True
    )


def of_everyone(shard, axis):
    everything = sent_to_all(shard, axis)
    return jnp.sum(everything, axis=0)


def with_halo(block, sides, width):
    for axis, dim in sides:
        count = lax.axis_size(axis)
        forward = [(i, i + 1) for i in range(count - 1)]
        backward = [(target, source) for source, target in forward]
        low = lax.ppermute(
            lax.slice_in_dim(block, block.shape[dim] - width, None, axis=dim), axis, forward
        )
        high = lax.ppermute(lax.slice_in_dim(block, 0, width, axis=dim), axis, backward)
        block = jnp.concatenate([low, block, high], axis=dim)
    return block


def north_table(order_ints, degree_count, theta_count):
    half_rows = theta_count // 2
    row_index = jnp.arange(half_rows, dtype=jnp.float32)
    angles = jnp.pi * (row_index + 0.5) / theta_count
    cosine = jnp.cos(angles)
    sine_theta = jnp.sin(angles)
    order_float = order_ints.astype(jnp.float32)[:, None]
    steps_k = jnp.arange(1, degree_count, dtype=jnp.int32)
    steps_float = steps_k.astype(jnp.float32)
    log_terms = 0.5 * jnp.log((2.0 * steps_float + 1.0) / (2.0 * steps_float))
    log_taken = jnp.where(steps_k[None, :] <= order_ints[:, None], log_terms[None, :], 0.0)
    log_start = 0.5 * jnp.log(jnp.float32(0.5)) + jnp.sum(log_taken, axis=1)
    log_sector = log_start[:, None] + order_float * jnp.log(sine_theta)[None, :]
    sectoral = jnp.exp(jnp.maximum(log_sector, -60.0))
    unscale = jnp.exp(jnp.minimum(log_sector + 60.0, 0.0))
    order_col = order_ints[:, None]
    blocks = 16
    per_block = degree_count // blocks

    def advance(state_pair, block_index):
        latest, before = state_pair
        produced = []
        for inner_step in range(per_block):
            degree = block_index * per_block + inner_step
            degree_float = degree.astype(jnp.float32)
            general = degree > order_col + 1
            degree_square = degree_float * degree_float
            order_square = order_float * order_float
            ratio_upper = jnp.where(
                general,
                (4.0 * degree_square - 1.0) / jnp.where(general, degree_square - order_square, 1.0),
                1.0,
            )
            lower_degree = degree_float - 1.0
            ratio_lower = jnp.where(
                general,
                (lower_degree * lower_degree - order_square)
                / (4.0 * lower_degree * lower_degree - 1.0),
                0.0,
            )
            value_general = jnp.sqrt(ratio_upper) * (
                cosine[None, :] * latest - jnp.sqrt(ratio_lower) * before
            )
            first_up = jnp.sqrt(2.0 * order_float + 3.0) * cosine[None, :] * sectoral
            new_value = jnp.where(
                degree < order_col,
                0.0,
                jnp.where(
                    degree == order_col,
                    sectoral,
                    jnp.where(degree == order_col + 1, first_up, value_general),
                ),
            )
            before = latest
            latest = new_value
            produced.append(new_value)
        return ((latest, before), jnp.stack(produced))

    zero_rows = jnp.zeros((order_ints.shape[0], half_rows), jnp.float32)
    state_pair, legendre_raw = lax.scan(
        advance, (zero_rows, zero_rows), jnp.arange(blocks, dtype=jnp.int32)
    )
    legendre_raw = legendre_raw.reshape(degree_count, order_ints.shape[0], half_rows)
    return jnp.transpose(legendre_raw, (1, 0, 2)) * unscale[:, None, :]


def full_table(north_rows, order_ints):
    degree_count = north_rows.shape[1]
    degrees = jnp.arange(degree_count, dtype=jnp.int32)
    parity = (degrees[None, :] + order_ints[:, None]) % 2
    sign_factor = (1 - 2 * parity).astype(jnp.float32)[:, :, None]
    return jnp.concatenate([north_rows, sign_factor * jnp.flip(north_rows, 2)], 2)


def quadrature(theta_count):
    half_rows = theta_count // 2
    row_index = jnp.arange(half_rows, dtype=jnp.float32)
    angles = jnp.pi * (row_index + 0.5) / theta_count
    wave_number = jnp.arange(1, half_rows + 1, dtype=jnp.float32)
    series = jnp.cos(2.0 * wave_number[None, :] * angles[:, None]) / (
        4.0 * wave_number[None, :] * wave_number[None, :] - 1.0
    )
    north_weights = 2.0 / theta_count * (1.0 - 2.0 * jnp.sum(series, axis=1))
    return jnp.concatenate([north_weights, jnp.flip(north_weights, 0)], 0)


def trig_table(degree_count, phi_count):
    orders = jnp.arange(degree_count, dtype=jnp.int32)[:, None]
    points = jnp.arange(phi_count, dtype=jnp.int32)[None, :]
    phase_angle = 2.0 * jnp.pi * (orders * points % phi_count).astype(jnp.float32) / phi_count
    return jnp.stack([jnp.cos(phase_angle), jnp.sin(phase_angle)]).astype(jnp.bfloat16)


def analysis_factor(order_ints, row_weights, degree_count, phi_count):
    mode_weight = jnp.where(order_ints == 0, 1.0, 2.0).astype(jnp.float32)
    return mode_weight[:, None] * float(degree_count) * row_weights[None, :] / float(phi_count)


def energy_weights(order_ints, degree_count):
    degrees = jnp.arange(degree_count, dtype=jnp.int32)
    order_col = order_ints[:, None]
    live_part = (degrees[None, :] >= order_col).astype(jnp.float32)
    inverse_modes = 1.0 / (2.0 * degrees.astype(jnp.float32) + 1.0)
    cosine_weight = jnp.where(order_col == 0, 0.5, 1.0)
    sine_weight = jnp.where(order_col == 0, 0.0, 1.0)
    return jnp.stack(
        [
            cosine_weight * live_part * inverse_modes[None, :],
            sine_weight * live_part * inverse_modes[None, :],
        ]
    )


def cross_product(first_vec, second_vec):
    return [
        first_vec[1] * second_vec[2] - first_vec[2] * second_vec[1],
        first_vec[2] * second_vec[0] - first_vec[0] * second_vec[2],
        first_vec[0] * second_vec[1] - first_vec[1] * second_vec[0],
    ]


def nonlinear_terms(components):
    velocity_vec = components[0:3]
    magnetic_vec = components[3:6]
    vorticity_vec = components[6:9]
    current_vec = components[9:12]
    lamb_term = cross_product(velocity_vec, vorticity_vec)
    lorentz_term = cross_product(current_vec, magnetic_vec)
    induced = cross_product(velocity_vec, magnetic_vec)
    return [lamb_term[index_c] + lorentz_term[index_c] for index_c in range(3)] + induced


def combine_terms(grid_values):
    components = [grid_values[:, index_c] for index_c in range(12)]
    return jnp.stack(nonlinear_terms(components), 1).astype(jnp.bfloat16)


def local(velocity, magnetic, vorticity, current):
    harm_count = lax.axis_size("harm")
    harm_index = lax.axis_index("harm")
    shell_count = velocity.shape[1]
    local_modes = velocity.shape[3]
    degree_count = velocity.shape[4]
    theta_count = 3 * degree_count // 2
    phi_count = 3 * degree_count
    row_count = theta_count // harm_count
    local_order = harm_index * local_modes + jnp.arange(local_modes, dtype=jnp.int32)
    all_orders = jnp.arange(degree_count, dtype=jnp.int32)
    north_rows = north_table(local_order, degree_count, theta_count)
    legendre_full = full_table(north_rows, local_order).astype(jnp.bfloat16)
    trig_rows = trig_table(degree_count, phi_count)
    row_weights = lax.dynamic_slice_in_dim(
        quadrature(theta_count), harm_index * row_count, row_count
    )
    analysis_scale = analysis_factor(all_orders, row_weights, degree_count, phi_count)
    energy_weight = energy_weights(local_order, degree_count)
    kinetic = jnp.sum(velocity.astype(jnp.float32) ** 2 * energy_weight[None, None], axis=(0, 2, 3))
    magnetic_energy = jnp.sum(
        magnetic.astype(jnp.float32) ** 2 * energy_weight[None, None], axis=(0, 2, 3)
    )
    energy = of_everyone(jnp.stack([kinetic, magnetic_energy]), "harm")
    spectrum = jnp.concatenate([velocity, magnetic, vorticity, current], 0).reshape(
        -1, local_modes, degree_count
    )
    summed = jnp.einsum("kml,mlt->mtk", spectrum, legendre_full, preferred_element_type=jnp.float32)
    mode_rows = (summed * (1.0 / degree_count)).astype(jnp.bfloat16)
    arrived = lax.all_to_all(
        mode_rows.reshape(local_modes, harm_count, row_count, -1),
        "harm",
        split_axis=1,
        concat_axis=0,
        tiled=True,
    )
    item_count = arrived.shape[2]
    shaped = arrived.reshape(degree_count, item_count, 12, shell_count, 2)
    products = combine_terms(
        jnp.einsum("mtcsr,rmp->tcsp", shaped, trig_rows, preferred_element_type=jnp.float32)
    )
    analysed = jnp.einsum(
        "tcsp,rmp->mtcsr", products, trig_rows, preferred_element_type=jnp.float32
    )
    analysed = (
        (analysed * analysis_scale[:, :, None, None, None])
        .astype(jnp.bfloat16)
        .reshape(degree_count, row_count, -1)
    )
    spectra = jnp.einsum(
        "mtk,mlt->kml",
        lax.all_to_all(analysed, "harm", split_axis=0, concat_axis=1, tiled=True),
        legendre_full,
        preferred_element_type=jnp.float32,
    )
    spectra = spectra.reshape(6, shell_count, 2, local_modes, degree_count)
    advection = spectra[:3].astype(jnp.bfloat16)
    induction = spectra[3:].astype(jnp.bfloat16)
    rimmed = with_halo(induction, (("rad", 1),), 1)
    gradient = (
        (rimmed[:, 2:].astype(jnp.float32) - rimmed[:, :-2].astype(jnp.float32)) * 0.5
    ).astype(jnp.bfloat16)
    return (advection, gradient, energy)


def solution(mesh):
    return jax.shard_map(
        local,
        mesh=mesh,
        in_specs=(
            P(None, "rad", None, "harm", None),
            P(None, "rad", None, "harm", None),
            P(None, "rad", None, "harm", None),
            P(None, "rad", None, "harm", None),
        ),
        out_specs=(
            P(None, "rad", None, "harm", None),
            P(None, "rad", None, "harm", None),
            P(None, "rad", None),
        ),
        check_vma=False,
    )
```

profile of v0, /device:TPU:7, one launch (start us, length us, event | category | flops | bytes accessed | tf_op | source)
XLA Modules:
  0.0 196.6 jit_solution(8778389006801127100)
XLA Ops:
  1.1 70.3 %while.21 = (s32[]{:T(128)}, f32[8,192]{1,0:T(8,128)S(1)}, f32[8,192]{1,0:T(8,128)S(1)}, f32[16,16,8,192]{3,1,0,2:T(8,128)}, s32[16]{0:T(128)S(1)}, /*index=5*/s...) while((s32[]{:T(128)}, f32[8,192]{1,0:T(8,128)S(1)}, ...), condition=%wide.region_2.3_spmd.clone.clone.clone.clone, body=%wide.region_1.2_spmd.clone.clone.clone.clone.sunk | while | flops 302466 | bytes 848968 | solution.py:91
  18.0 0.7 copy_dynamic-update-slice_fusion.2
  22.4 0.7 copy_dynamic-update-slice_fusion.2
  35.5 0.7 copy_dynamic-update-slice_fusion.2
  48.7 0.7 copy_dynamic-update-slice_fusion.2
  70.6 0.7 copy_dynamic-update-slice_fusion.2
  71.4 1.9 bitcast_convert_fusion
  73.2 11.6 %reverse.6 = f32[8,256,256]{2,1,0:T(8,128)} reverse(f32[8,256,256]{2,1,0:T(8,128)S(1)} %bitcast.583), dimensions={2} | reverse | bytes 4194304
  84.9 2.5 %multiply_convert_fusion = bf16[8,256,192]{2,1,0:T(8,128)(2,1)S(1)} fusion(f32[8,256]{1,0:T(8,128)S(1)} %fusion.102, f32[8,256,256]{2,1,0:T(8,128)} %reverse.6), kind=kLoop, calls=%fused_computation.197 | loop fusion | flops 786432 | bytes 2367488 | tf_op jit(solution)/shard_map/convert.11
  87.5 0.9 copy-done
  89.1 1.4 copy.64
  90.5 12.8 %all-to-all-start = ((bf16[8,32,12,96]{3,0,2,1:T(8,128)(2,1)}), bf16[8,32,12,96]{3,0,2,1:T(8,128)(2,1)S(1)}, u32[]{:S(2)}, u32[]{:S(2)}) async-start(bf16[8,32,12,96]{3,0,2,1:T(8,128)(2,1)} %bitcast.5), calls=%async_computation | async-start | bytes 1572864 | tf_op jit(solution)/shard_map/all_to_all | solution.py:198
  103.4 0.8 fusion.98
  104.5 3.4 %sine_convert_fusion = (bf16[1,256,768]{2,1,0:T(8,128)(2,1)S(1)}, bf16[1,256,768]{2,1,0:T(8,128)(2,1)S(1)}) fusion(), kind=kLoop, calls=%fused_computation.215 | loop fusion | flops 2162688 | bytes 786432 | tf_op jit(solution)/shard_map/convert.9
  108.0 16.7 %all-to-all-done = bf16[8,32,12,96]{3,0,2,1:T(8,128)(2,1)S(1)} async-done(((bf16[8,32,12,96]{3,0,2,1:T(8,128)(2,1)}), bf16[8,32,12,96]{3,0,2,1:T(8,128)(2,1)S(1)}, u32[]{:S(2)}, u32[]{:S(2)}) %all-to-all-start) | async-done | bytes 589856 | tf_op jit(solution)/shard_map/all_to_all | solution.py:198
  124.7 8.3 %copy.65 = bf16[32,8,1,12,96]{1,0,4,3,2:T(8,128)(2,1)} copy(bf16[32,8,1,12,96]{4,1,3,0,2:T(8,128)(2,1)S(1)} %bitcast.586) | data formatting | bytes 1179648 | tf_op jit(solution)/shard_map/all_to_all | solution.py:198
  133.0 12.6 %reshape.1511 = bf16[256,12,12,4,2]{0,4,3,2,1:T(2,128)(2,1)S(1)} reshape(bf16[32,8,1,12,96]{1,0,4,3,2:T(8,128)(2,1)} %copy.65) | data formatting | bytes 1179648 | tf_op jit(solution)/shard_map/reshape | solution.py:206
  145.5 0.8 convolution_bitcast_fusion
  146.3 1.3 subtract_convert_fusion
  147.6 1.1 subtract_convert_fusion.2
  148.7 0.8 add_convert_fusion.2
  149.5 1.4 stack.150
  151.9 0.9 copy.69
  152.9 2.0 reshape.1516
  154.9 6.3 %all-to-all-start.1 = ((bf16[32,2,2304]{2,1,0:T(2,128)(2,1)}), bf16[32,2,2304]{2,1,0:T(2,128)(2,1)S(1)}, u32[]{:S(2)}, u32[]{:S(2)}) async-start(bf16[32,2,2304]{2,1,0:T(2,128)(2,1)} %reshape.1516), calls=%async_computation.1 | async-start | bytes 589824 | tf_op jit(solution)/shard_map/all_to_all | solution.py:220
  161.4 12.5 %all-to-all-done.1 = bf16[32,2,2304]{2,1,0:T(2,128)(2,1)S(1)} async-done(((bf16[32,2,2304]{2,1,0:T(2,128)(2,1)}), bf16[32,2,2304]{2,1,0:T(2,128)(2,1)S(1)}, u32[]{:S(2)}, u32[]{:S(2)}) %all-to-all-start.1) | async-done | bytes 294944 | tf_op jit(solution)/shard_map/all_to_all | solution.py:220
  173.9 0.7 broadcast_in_dim.677
  174.6 4.8 %all-to-all-start.2 = ((f32[32,2,4,256]{3,2,1,0:T(4,128)}), f32[32,2,4,256]{3,2,1,0:T(4,128)S(1)}, u32[]{:S(2)}, u32[]{:S(2)}) async-start(f32[32,2,4,256]{3,2,1,0:T(4,128)} %broadcast_in_dim.677), calls=%async_computation.2 | async-start | bytes 524288 | tf_op jit(solution)/shard_map/all_to_all | solution.py:9
  179.4 1.3 reshape.1517
  180.9 2.0 %fusion.85 = bf16[48,8,256]{2,0,1:T(8,128)(2,1)S(1)} fusion(bf16[8,384,48]{2,0,1:T(8,128)(2,1)S(1)} %bitcast.587, bf16[8,256,192]{2,1,0:T(8,128)(2,1)} %copy-done, bf16[8,256,192]{2,1,0:T(8,128)(2,1)S(1)} %get-tuple-element.483), kind=kOutput, calls=%fused_computation.207 | convolution fusion | flops 78741504 | bytes 2064384 | tf_op jit(solution)/shard_map/mtk,mlt->kml/dot_general | solution.py:218
  183.0 3.6 %collective-permute-start = (bf16[3,1,2,8,256]{4,3,2,1,0:T(8,128)(2,1)S(1)}, bf16[3,1,2,8,256]{4,3,2,1,0:T(8,128)(2,1)S(1)}, u32[]{:S(2)}, u32[]{:S(2)}) collective-permute-start(bf16[3,1,2,8,256]{4,3,2,1,0:T(8,128)(2,1)S(1)} %get-tuple-element.572), channel_id=1, source_target_pairs={{32,0},{64,32},{96,64},{128,96},{160,128},{192,160},{224,192},{256... | collective-permute-start | bytes 73736 | tf_op jit(solution)/shard_map/ppermute | solution.py:27
  186.7 7.9 %collective-permute-start.1 = (bf16[3,1,2,8,256]{4,3,2,1,0:T(8,128)(2,1)S(1)}, bf16[3,1,2,8,256]{4,3,2,1,0:T(8,128)(2,1)S(1)}, u32[]{:S(2)}, u32[]{:S(2)}) collective-permute-start(bf16[3,1,2,8,256]{4,3,2,1,0:T(8,128)(2,1)S(1)} %get-tuple-element.573), channel_id=1, source_target_pairs={{0,32},{32,64},{64,96},{96,128},{128,160},{160,192},{192,224},{224... | collective-permute-start | bytes 73736 | tf_op jit(solution)/shard_map/ppermute | solution.py:24
  (1008 shorter events, 52.5 us)
Async XLA Ops:
  84.8 2.5 %copy-start.1 = (bf16[3,4,2,8,256]{4,3,2,1,0:T(8,128)(2,1)S(1)}, bf16[3,4,2,8,256]{4,3,2,1,0:T(8,128)(2,1)}, u32[]{:S(2)}) copy-start(bf16[3,4,2,8,256]{4,3,2,1,0:T(8,128)(2,1)} %param.7) | copy-start | bytes 294916
  84.8 2.5 %copy-start.2 = (bf16[3,4,2,8,256]{4,3,2,1,0:T(8,128)(2,1)S(1)}, bf16[3,4,2,8,256]{4,3,2,1,0:T(8,128)(2,1)}, u32[]{:S(2)}) copy-start(bf16[3,4,2,8,256]{4,3,2,1,0:T(8,128)(2,1)} %param.6) | copy-start | bytes 294916
  84.9 2.6 %copy-start.4 = (bf16[3,4,2,8,256]{4,3,2,1,0:T(8,128)(2,1)S(1)}, bf16[3,4,2,8,256]{4,3,2,1,0:T(8,128)(2,1)}, u32[]{:S(2)}) copy-start(bf16[3,4,2,8,256]{4,3,2,1,0:T(8,128)(2,1)} %param.9) | copy-start | bytes 294916
  84.9 2.6 %copy-start.5 = (bf16[3,4,2,8,256]{4,3,2,1,0:T(8,128)(2,1)S(1)}, bf16[3,4,2,8,256]{4,3,2,1,0:T(8,128)(2,1)}, u32[]{:S(2)}) copy-start(bf16[3,4,2,8,256]{4,3,2,1,0:T(8,128)(2,1)} %param.8) | copy-start | bytes 294916
  87.4 1.0 copy-start
  90.5 34.2 %all-to-all-start = ((bf16[8,32,12,96]{3,0,2,1:T(8,128)(2,1)}), bf16[8,32,12,96]{3,0,2,1:T(8,128)(2,1)S(1)}, u32[]{:S(2)}, u32[]{:S(2)}) async-start(bf16[8,32,12,96]{3,0,2,1:T(8,128)(2,1)} %bitcast.5), calls=%async_computation | async-start | bytes 1572864 | tf_op jit(solution)/shard_map/all_to_all | solution.py:198
  151.8 9.5 %copy-start.3 = (bf16[3,4,2,8,256]{4,3,2,1,0:T(8,128)(2,1)S(1)}, bf16[3,4,2,8,256]{4,3,2,1,0:T(8,128)(2,1)}, u32[]{:S(2)}) copy-start(bf16[3,4,2,8,256]{4,3,2,1,0:T(8,128)(2,1)} %param.6) | copy-start | bytes 294916
  154.9 19.0 %all-to-all-start.1 = ((bf16[32,2,2304]{2,1,0:T(2,128)(2,1)}), bf16[32,2,2304]{2,1,0:T(2,128)(2,1)S(1)}, u32[]{:S(2)}, u32[]{:S(2)}) async-start(bf16[32,2,2304]{2,1,0:T(2,128)(2,1)} %reshape.1516), calls=%async_computation.1 | async-start | bytes 589824 | tf_op jit(solution)/shard_map/all_to_all | solution.py:220
  174.6 20.0 %all-to-all-start.2 = ((f32[32,2,4,256]{3,2,1,0:T(4,128)}), f32[32,2,4,256]{3,2,1,0:T(4,128)S(1)}, u32[]{:S(2)}, u32[]{:S(2)}) async-start(f32[32,2,4,256]{3,2,1,0:T(4,128)} %broadcast_in_dim.677), calls=%async_computation.2 | async-start | bytes 524288 | tf_op jit(solution)/shard_map/all_to_all | solution.py:9
  183.0 12.9 %collective-permute-start = (bf16[3,1,2,8,256]{4,3,2,1,0:T(8,128)(2,1)S(1)}, bf16[3,1,2,8,256]{4,3,2,1,0:T(8,128)(2,1)S(1)}, u32[]{:S(2)}, u32[]{:S(2)}) collective-permute-start(bf16[3,1,2,8,256]{4,3,2,1,0:T(8,128)(2,1)S(1)} %get-tuple-element.572), channel_id=1, source_target_pairs={{32,0},{64,32},{96,64},{128,96},{160,128},{192,160},{224,192},{256... | collective-permute-start | bytes 73736 | tf_op jit(solution)/shard_map/ppermute | solution.py:27
  186.7 9.3 %collective-permute-start.1 = (bf16[3,1,2,8,256]{4,3,2,1,0:T(8,128)(2,1)S(1)}, bf16[3,1,2,8,256]{4,3,2,1,0:T(8,128)(2,1)S(1)}, u32[]{:S(2)}, u32[]{:S(2)}) collective-permute-start(bf16[3,1,2,8,256]{4,3,2,1,0:T(8,128)(2,1)S(1)} %get-tuple-element.573), channel_id=1, source_target_pairs={{0,32},{32,64},{64,96},{96,128},{128,160},{160,192},{192,224},{224... | collective-permute-start | bytes 73736 | tf_op jit(solution)/shard_map/ppermute | solution.py:24
where the time goes:
time: 197 us
  local copies, waits for them, and re-layouts  63.4 us (32%)
  other arithmetic  44.4 us (23%)
  starting transfers between devices  35.5 us (18%)
  waiting for transfers between devices  29.2 us (15%)
  loops' own time  19.1 us (10%)
  matrix products  4.02 us (2%)
    while x240, other arithmetic  20.3 us
    another operation x1, loops' own time, north_table(): lax.scan(advance, (zero_rows, zero_rows), jnp.arange(blocks, dtype=jnp.in...  19.1 us
    all_to_all x1, waiting for transfers between devices, local(): lax.all_to_all(mode_rows.reshape(local_modes, harm_count, row_count, -1),...  16.7 us
    unnamed x17, local copies, waits for them, and re-layouts  16.6 us
    all_to_all x1, starting transfers between devices, local(): lax.all_to_all(mode_rows.reshape(local_modes, harm_count, row_count, -1),...  12.8 us
    reshape x1, local copies, waits for them, and re-layouts, local(): shaped = arrived.reshape(degree_count, item_count, 12, shell_count, 2)  12.6 us
    all_to_all x1, waiting for transfers between devices, local(): lax.all_to_all(analysed, 'harm', split_axis=0, concat_axis=1, tiled=True)  12.5 us
    dynamic_update_slice x16, local copies, waits for them, and re-layouts, north_table(): lax.scan(advance, (zero_rows, zero_rows), jnp.arange(blocks, dtype=jnp.in...  11.4 us
  transfers between devices with their start and end apart: 5, of which 2 were waited for; matrix products, arithmetic and copies ran while one was open for 5% of the time, Pallas kernels for 0%

commit v1 on v0

v1 whole, which is shorter than its diff:
```python
import functools

import jax
import jax.numpy as jnp
from jax import lax
from jax.experimental import pallas as pl
from jax.experimental.pallas import tpu as pltpu
from jax.sharding import PartitionSpec as P

F32 = jnp.float32
BF16 = jnp.bfloat16
PI = 3.14159265358979
L = 256
HARM = 32
RAD = 16
NPHI = 768
CROW = 64


def sin_poly(y):
    z = y * y
    s = -1.0 / 39916800.0
    for c in (1.0 / 362880.0, -1.0 / 5040.0, 1.0 / 120.0, -1.0 / 6.0, 1.0):
        s = s * z + c
    return y * s


def cos_768(q):
    return sin_poly((192.0 - jnp.minimum(q, 768.0 - q)) * (PI / 384.0))


def mod_768(v):
    return v - 768.0 * jnp.floor((v + 0.5) * (1.0 / 768.0))


def iota(shape, dim):
    return lax.broadcasted_iota(jnp.int32, shape, dim)


def fiota(shape, dim):
    return iota(shape, dim).astype(F32)


def parity_sign(order):
    return 1.0 - 2.0 * ((iota((1, L), 1) + order) & 1).astype(F32)


def legendre_steps(me, tab):
    order = (me * 8 + iota((8, 128), 0)).astype(F32)
    order_sq = order * order
    degree = fiota((8, L), 1)
    own = (me * 8 + iota((8, L), 0)).astype(F32)
    logs = 0.5 * jnp.log((2.0 * degree + 1.0) / jnp.maximum(2.0 * degree, 1.0))
    taken = jnp.where((degree >= 1.0) & (degree <= own), logs, 0.0)
    log_start = 0.5 * jnp.log(jnp.full((8, 1), 0.5, F32)) + jnp.sum(taken, axis=1, keepdims=True)
    cosine, sector, unscale = [], [], []
    for jt in range(2):
        odd = 2.0 * (fiota((8, 128), 1) + 128.0 * jt) + 1.0
        cosine.append(sin_poly((384.0 - odd) * (PI / 768.0)))
        sine = sin_poly(jnp.minimum(odd, 768.0 - odd) * (PI / 768.0))
        log_sector = log_start + order * jnp.log(sine)
        sector.append(jnp.exp(jnp.maximum(log_sector, -60.0)))
        unscale.append(jnp.exp(jnp.minimum(log_sector + 60.0, 0.0)))
    zero = jnp.zeros((8, 128), F32)
    per = 16

    def block(index, state):
        q0, p0, q1, p1, back = state
        for inner in range(per):
            deg_i = index * per + inner
            deg = deg_i.astype(F32)
            sq = deg * deg
            live = order < deg
            t = (4.0 * sq - 1.0) / jnp.where(live, sq - order_sq, 1.0)
            a = jnp.where(live, jnp.sqrt(t), 0.0)
            ab = a * back
            back = jnp.where(live, lax.rsqrt(t), 0.0)
            start = order == deg
            n0 = a * cosine[0] * q0 + (jnp.where(start, sector[0], 0.0) - ab * p0)
            n1 = a * cosine[1] * q1 + (jnp.where(start, sector[1], 0.0) - ab * p1)
            row = pl.ds(pl.multiple_of(deg_i * 8, 8), 8)
            tab[0, row, :] = n0 * unscale[0]
            tab[1, row, :] = n1 * unscale[1]
            q0, p0, q1, p1 = n0, q0, n1, q1
        return q0, p0, q1, p1, back

    lax.fori_loop(0, L // per, block, (zero, zero, zero, zero, zero))


def kernel(
    vel, mag, vor, cur,
    adv, grad, energy,
    tab, qt, coef, rhs, synth, wire, modes, trig, turned, grid, prod, spec, back, backf,
    zed, out, ind, low, high, esrc, erecv, ered, efin,
    mode_send, mode_recv, spec_send, spec_recv, halo_send, halo_recv, e_send, e_recv,
):
    me = lax.axis_index("harm")
    my_rad = lax.axis_index("rad")
    up = lax.rem(my_rad + 1, RAD)
    down = lax.rem(my_rad + RAD - 1, RAD)

    def peer(i):
        return lax.rem(me + i, HARM)

    barrier = pltpu.get_barrier_semaphore()

    def greet(i, carry):
        pl.semaphore_signal(barrier, inc=1, device_id={"harm": peer(i)})
        return carry

    lax.fori_loop(1, HARM, greet, 0)
    pl.semaphore_signal(barrier, inc=1, device_id={"rad": up})
    pl.semaphore_signal(barrier, inc=1, device_id={"rad": down})

    coef[:, 0:CROW, :] = jnp.zeros((2, CROW, 128), F32)
    coef[:, CROW + 768:, :] = jnp.zeros((2, CROW, 128), F32)
    for a, ref in enumerate((vel, mag, vor, cur)):
        for half in range(2):
            lanes = pl.ds(half * 128, 128)
            coef[half, CROW + 192 * a:CROW + 192 * (a + 1), :] = (
                ref[:, :, :, :, lanes].astype(F32).reshape(192, 128)
            )

    legendre_steps(me, tab)

    row8 = iota((8, 128), 0)

    def synthesis(m, carry):
        for jt, rows in ((0, 128), (1, 64)):
            table = tab[jt, pl.ds(m, L, stride=8), :]
            qt[m, jt * 128:jt * 128 + rows, :] = table.T[0:rows].astype(BF16)
        sign = parity_sign(m)
        for r in range(2):
            for half in range(2):
                sgn = sign[:, half * 128:(half + 1) * 128]
                before = None
                for c in range(-1, 12):
                    rows = coef[half, pl.ds(CROW + c * 64 + r * 8 + m, 8, stride=16), :]
                    if c >= 0:
                        base = r * 192 + c * 16
                        for gn, part in ((0, jnp.where(row8 < 4, rows, 0.0)),
                                         (1, jnp.where(row8 >= 4, before, 0.0))):
                            lane = gn * 256 + half * 128
                            rhs[base:base + 16, lane:lane + 128] = jnp.concatenate(
                                [part, part * sgn], axis=0
                            ).astype(BF16)
                    before = rows
        lhs = jnp.concatenate([qt[m, 0:96, :], qt[m, 96:192, :]], axis=1)
        made = lax.dot_general(
            lhs, rhs[...], (((1,), (1,)), ((), ())), preferred_element_type=F32
        ) * (1.0 / L)
        for k in range(3):
            for lt in range(3):
                synth[k, lt, pl.ds(m, 32, stride=8), :] = made[
                    k * 32:(k + 1) * 32, lt * 128:(lt + 1) * 128
                ]
        return carry

    lax.fori_loop(0, 8, synthesis, 0)
    wire[...] = synth[...].astype(BF16)

    pl.semaphore_wait(barrier, HARM + 1)

    def rows_of(device):
        return pl.ds(pl.multiple_of(device * 8, 8), 8)

    def mode_copy(k, i):
        to = peer(i)
        return pltpu.make_async_remote_copy(
            src_ref=wire.at[k, :, rows_of(to), :],
            dst_ref=modes.at[k, :, rows_of(me), :],
            send_sem=mode_send.at[k],
            recv_sem=mode_recv.at[k],
            device_id={"harm": to},
        )

    for k in range(3):
        def send_modes(i, carry, k=k):
            mode_copy(k, i).start()
            return carry

        lax.fori_loop(1, HARM, send_modes, 0)
        pltpu.make_async_copy(
            wire.at[k, :, rows_of(me), :], modes.at[k, :, rows_of(me), :], mode_recv.at[k]
        ).start()

    order8 = me * 8 + iota((8, 128), 0)
    for half in range(2):
        degree = iota((8, 128), 1) + 128 * half
        weight = jnp.where(degree >= order8, 1.0 / (2.0 * degree.astype(F32) + 1.0), 0.0)
        weights = (
            weight * jnp.where(order8 == 0, 0.5, 1.0),
            weight * jnp.where(order8 == 0, 0.0, 1.0),
        )
        for q in range(2):
            for s in range(4):
                total = jnp.zeros((8, 128), F32)
                for c in range(3):
                    for r in range(2):
                        at = CROW + (((q * 3 + c) * 4 + s) * 2 + r) * 8
                        value = coef[half, at:at + 8, :]
                        total += value * value * weights[r]
                esrc[(q * 4 + s) * 2 + half] = jnp.sum(total, axis=0, keepdims=True)

    def energy_copy(i):
        to = peer(i)
        return pltpu.make_async_remote_copy(
            src_ref=esrc.at[lax.rem(to, 16)],
            dst_ref=erecv.at[me],
            send_sem=e_send.at[0],
            recv_sem=e_recv.at[0],
            device_id={"harm": to},
        )

    def send_energy(i, carry):
        energy_copy(i).start()
        return carry

    lax.fori_loop(1, HARM, send_energy, 0)
    pltpu.make_async_copy(esrc.at[lax.rem(me, 16)], erecv.at[me], e_recv.at[0]).start()

    def trig_rows(b, carry):
        angle = mod_768((b * 8 + iota((8, NPHI), 0)).astype(F32) * fiota((8, NPHI), 1))
        rows = pl.ds(pl.multiple_of(b * 8, 8), 8)
        trig[0, rows, :] = cos_768(angle).astype(BF16)
        trig[1, rows, :] = cos_768(jnp.where(angle >= 192.0, angle - 192.0, angle + 576.0)).astype(BF16)
        return carry

    lax.fori_loop(0, 32, trig_rows, 0)

    lane = iota((1, 128), 1)
    factors = []
    for k in range(3):
        row = ((lane >> 2) & 1) * 96 + k * 32 + me
        wave = fiota((192, 128), 0) + 1.0
        odd = (2 * row + 1).astype(F32)
        series = cos_768(mod_768(wave * odd)) / (4.0 * wave * wave - 1.0)
        weight = (2.0 / 384.0) * (1.0 - 2.0 * jnp.sum(series, axis=0, keepdims=True))
        factors.append(weight * (256.0 / 768.0))

    def grid_of(k):
        for lt in range(3):
            turned[lt * 128:(lt + 1) * 128, :] = modes[k, lt].T
        grid[...] = jnp.dot(turned[0:192], trig[0], preferred_element_type=F32) + jnp.dot(
            turned[192:384], trig[1], preferred_element_type=F32
        )
        for pt in range(6):
            cols = slice(pt * 128, (pt + 1) * 128)
            g = [grid[c * 16:(c + 1) * 16, cols] for c in range(12)]
            u, b, w, j = g[0:3], g[3:6], g[6:9], g[9:12]

            def cross(x, y, i):
                n, o = (i + 1) % 3, (i + 2) % 3
                return x[n] * y[o] - x[o] * y[n]

            for c in range(6):
                value = cross(u, w, c) + cross(j, b, c) if c < 3 else cross(u, b, c - 3)
                value = value.astype(BF16)
                ends = (96, ) if c < 2 else (128 - 32, 192 - 32)
                prod[c * 16:(c + 1) * 16, cols] = value
                for end in ends:
                    prod[end + c * 16:end + (c + 1) * 16, cols] = value

    even = iota((256, 1), 0)
    mode_weight = jnp.where(even == 0, 1.0, 2.0)
    wide_lane = iota((1, 128), 1)

    def analysed(k):
        cosine = lax.dot_general(
            trig[0], prod[0:128], (((1,), (1,)), ((), ())), preferred_element_type=F32
        )
        sine = lax.dot_general(
            trig[1], prod[...], (((1,), (1,)), ((), ())), preferred_element_type=F32
        )
        scale = mode_weight * factors[k]
        first = jnp.where(wide_lane < 96, cosine, sine[:, 0:128]) * scale
        second = sine[:, 128:256] * scale
        return first.astype(BF16), second

    def wait_modes(k):
        pltpu.make_async_copy(modes.at[k], modes.at[k], mode_recv.at[k]).wait()

    def spec_copy(part, tiles, i):
        to = peer(i)
        return pltpu.make_async_remote_copy(
            src_ref=spec.at[tiles, rows_of(to), :],
            dst_ref=back.at[tiles, rows_of(me), :],
            send_sem=spec_send.at[part],
            recv_sem=spec_recv.at[part],
            device_id={"harm": to},
        )

    def send_spectra(part, tiles):
        def one(i, carry):
            spec_copy(part, tiles, i).start()
            return carry

        lax.fori_loop(1, HARM, one, 0)
        pltpu.make_async_copy(
            spec.at[tiles, rows_of(me), :], back.at[tiles, rows_of(me), :], spec_recv.at[part]
        ).start()

    tiles_a, tiles_b = pl.ds(0, 3), pl.ds(3, 2)
    wait_modes(0)
    grid_of(0)
    first, second0 = analysed(0)
    spec[0] = first
    spec[1] = second0.astype(BF16)
    wait_modes(1)
    grid_of(1)
    first, second1 = analysed(1)
    spec[2] = first
    spec[1] = jnp.where(wide_lane < 64, spec[1].astype(F32), second1).astype(BF16)
    send_spectra(0, tiles_a)

    pltpu.make_async_copy(erecv, erecv, e_recv.at[0]).wait()
    ered[...] = jnp.sum(erecv[...], axis=0, keepdims=True)
    mine = lax.rem(me, 16)

    def row_copy(i):
        to = me - mine + lax.rem(mine + i, 16)
        return pltpu.make_async_remote_copy(
            src_ref=ered.at[0],
            dst_ref=efin.at[mine],
            send_sem=e_send.at[1],
            recv_sem=e_recv.at[1],
            device_id={"harm": to},
        )

    def send_row(i, carry):
        row_copy(i).start()
        return carry

    lax.fori_loop(1, 16, send_row, 0)
    pltpu.make_async_copy(ered.at[0], efin.at[mine], e_recv.at[1]).start()

    wait_modes(2)
    grid_of(2)
    first, second2 = analysed(2)
    spec[3] = first
    spec[4] = second2.astype(BF16)
    send_spectra(1, tiles_b)

    def wait_spectra(part, tiles):
        pltpu.make_async_copy(back.at[tiles], back.at[tiles], spec_recv.at[part]).wait()

    wait_spectra(0, tiles_a)
    backf[0:3] = back[0:3].astype(F32)
    wait_spectra(1, tiles_b)
    backf[3:5] = back[3:5].astype(F32)

    lane_row = iota((32, 128), 1)
    gn_of = (lane_row >> 2) & 1

    def latitude(m, carry):
        tiles = [backf[t, pl.ds(m, 32, stride=8), :] for t in range(5)]
        middle = (
            jnp.where(lane_row < 64, tiles[1], 0.0),
            jnp.where(lane_row >= 64, tiles[1], 0.0),
            jnp.where(lane_row < 64, tiles[4], 0.0),
        )
        lead = (tiles[0], tiles[2], tiles[3])
        for gn in range(2):
            for k in range(3):
                at = (gn * 3 + k) * 32
                zed[at:at + 32, 0:128] = jnp.where(gn_of == gn, lead[k], 0.0).astype(BF16)
                zed[at:at + 32, 128:256] = jnp.where(gn_of == gn, middle[k], 0.0).astype(BF16)
        sums = lax.dot_general(
            zed[...], qt[m], (((0,), (0,)), ((), ())), preferred_element_type=F32
        )
        sums = jnp.concatenate([sums[0:128], sums[128:192] + sums[192:256]], axis=0)
        sign = parity_sign(m)
        for r in range(2):
            for c in range(6):
                base = r * 96 + c * 16
                both = sums[base:base + 8] + sums[base + 8:base + 16] * sign
                both = both[0:4] + both[4:8]
                for half in range(2):
                    out[half, pl.ds(c * 64 + r * 8 + m, 4, stride=16), :] = both[
                        :, half * 128:(half + 1) * 128
                    ]
        return carry

    lax.fori_loop(0, 8, latitude, 0)

    for half in range(2):
        lanes = pl.ds(half * 128, 128)
        ind[:, :, :, :, lanes] = out[half, 192:384, :].reshape(3, 4, 2, 8, 128).astype(BF16)

    to_up = pltpu.make_async_remote_copy(
        src_ref=ind.at[:, 3], dst_ref=low, send_sem=halo_send.at[0], recv_sem=halo_recv.at[0],
        device_id={"rad": up},
    )
    to_down = pltpu.make_async_remote_copy(
        src_ref=ind.at[:, 0], dst_ref=high, send_sem=halo_send.at[1], recv_sem=halo_recv.at[1],
        device_id={"rad": down},
    )
    to_up.start()
    to_down.start()

    for half in range(2):
        lanes = pl.ds(half * 128, 128)
        adv[:, :, :, :, lanes] = out[half, 0:192, :].reshape(3, 4, 2, 8, 128).astype(BF16)
    pltpu.make_async_copy(efin, efin, e_recv.at[1]).wait()
    for q in range(2):
        for s in range(4):
            for half in range(2):
                energy[q, s:s + 1, half * 128:(half + 1) * 128] = efin[(q * 4 + s) * 2 + half]

    shells = [ind[:, s].astype(F32) for s in range(4)]
    grad[:, 1] = ((shells[2] - shells[0]) * 0.5).astype(BF16)
    grad[:, 2] = ((shells[3] - shells[1]) * 0.5).astype(BF16)
    to_up.wait()
    to_down.wait()
    below = low[...].astype(F32) * jnp.where(my_rad == 0, 0.0, 1.0)
    above = high[...].astype(F32) * jnp.where(my_rad == RAD - 1, 0.0, 1.0)
    grad[:, 0] = ((shells[1] - below) * 0.5).astype(BF16)
    grad[:, 3] = ((above - shells[2]) * 0.5).astype(BF16)

    others = pl.ds(0, (HARM - 1) * 8)
    for k in range(3):
        sent = wire.at[k, :, others, :]
        pltpu.make_async_copy(sent, sent, mode_send.at[k]).wait()
    for part, tiles in ((0, tiles_a), (1, tiles_b)):
        sent = spec.at[tiles, others, :]
        pltpu.make_async_copy(sent, sent, spec_send.at[part]).wait()
    pltpu.make_async_copy(erecv.at[pl.ds(0, 31)], erecv.at[pl.ds(0, 31)], e_send.at[0]).wait()
    pltpu.make_async_copy(efin.at[pl.ds(0, 15)], efin.at[pl.ds(0, 15)], e_send.at[1]).wait()


def local(velocity, magnetic, vorticity, current):
    vmem = pl.BlockSpec(memory_space=pltpu.VMEM)
    block = velocity.shape
    return pl.pallas_call(
        kernel,
        out_shape=(
            jax.ShapeDtypeStruct(block, BF16),
            jax.ShapeDtypeStruct(block, BF16),
            jax.ShapeDtypeStruct((2, 4, L), F32),
        ),
        in_specs=[vmem] * 4,
        out_specs=(vmem,) * 3,
        scratch_shapes=[
            pltpu.VMEM((2, L * 8, 128), F32),
            pltpu.VMEM((8, 192, L), BF16),
            pltpu.VMEM((2, 768 + 2 * CROW, 128), F32),
            pltpu.VMEM((384, 512), BF16),
            pltpu.VMEM((3, 3, 256, 128), F32),
            pltpu.VMEM((3, 3, 256, 128), BF16),
            pltpu.VMEM((3, 3, 256, 128), BF16),
            pltpu.VMEM((2, 256, NPHI), BF16),
            pltpu.VMEM((384, 256), BF16),
            pltpu.VMEM((192, NPHI), F32),
            pltpu.VMEM((256, NPHI), BF16),
            pltpu.VMEM((5, 256, 128), BF16),
            pltpu.VMEM((5, 256, 128), BF16),
            pltpu.VMEM((5, 256, 128), F32),
            pltpu.VMEM((192, 256), BF16),
            pltpu.VMEM((2, 384, 128), F32),
            pltpu.VMEM((3, 4, 2, 8, L), BF16),
            pltpu.VMEM((3, 2, 8, L), BF16),
            pltpu.VMEM((3, 2, 8, L), BF16),
            pltpu.VMEM((16, 1, 128), F32),
            pltpu.VMEM((HARM, 1, 128), F32),
            pltpu.VMEM((1, 1, 128), F32),
            pltpu.VMEM((16, 1, 128), F32),
            pltpu.SemaphoreType.DMA((3,)),
            pltpu.SemaphoreType.DMA((3,)),
            pltpu.SemaphoreType.DMA((2,)),
            pltpu.SemaphoreType.DMA((2,)),
            pltpu.SemaphoreType.DMA((2,)),
            pltpu.SemaphoreType.DMA((2,)),
            pltpu.SemaphoreType.DMA((2,)),
            pltpu.SemaphoreType.DMA((2,)),
        ],
        compiler_params=pltpu.CompilerParams(collective_id=0, has_side_effects=True),
    )(velocity, magnetic, vorticity, current)


def solution(mesh):
    split = P(None, "rad", None, "harm", None)
    return jax.shard_map(
        local,
        mesh=mesh,
        in_specs=(split,) * 4,
        out_specs=(split, split, P(None, "rad", None)),
        check_vma=False,
    )
```

time: 197 us -> 53.7 us (0.27)
  local copies, waits for them, and re-layouts: 63.4 us -> 2.87 us
  Pallas kernels: 0 us -> 50 us
  other arithmetic: 44.4 us -> 0 us
  starting transfers between devices: 35.5 us -> 0 us
  waiting for transfers between devices: 29.2 us -> 0 us
  loops' own time: 19.1 us -> 0 us
  matrix products: 4.02 us -> 0 us
    pallas_call x0 -> x1, Pallas kernels: none -> 50 us  [local(): pl.pallas_call(kernel, out_shape=(jax.ShapeDtypeStruct(block, BF16), jax....]
    all_to_all x3 -> x0, waiting for transfers between devices: 29.2 us -> none  [the longest x1 16.7 us: local(): lax.all_to_all(mode_rows.reshape(local_modes, harm_count, row_count, -1),...]
    all_to_all x3 -> x0, starting transfers between devices: 23.9 us -> none  [the longest x1 12.8 us: local(): lax.all_to_all(mode_rows.reshape(local_modes, harm_count, row_count, -1),...]
    while x240 -> x0, other arithmetic: 20.3 us -> none
    another operation x1 -> x0, loops' own time: 19.1 us -> none  [north_table(): lax.scan(advance, (zero_rows, zero_rows), jnp.arange(blocks, dtype=jnp.in...]
    unnamed x17 -> x7, local copies, waits for them, and re-layouts: 16.6 us -> 2.87 us
    reshape x3 -> x0, local copies, waits for them, and re-layouts: 13.6 us -> none  [the longest x1 12.6 us: local(): shaped = arrived.reshape(degree_count, item_count, 12, shell_count, 2)]
    another operation x24 -> x0, other arithmetic: 12.3 us -> none
  transfers between devices with their start and end apart: 5 -> 0, of which waited for: 2 -> 0; matrix products, arithmetic and copies ran while one was open for 5% -> 0% of each run, Pallas kernels for 0% -> 0%
where the time goes in v1:
time: 53.7 us; the launch traced here: 53.5 us
  Pallas kernels  50 us (93%)
  local copies, waits for them, and re-layouts  2.87 us (5%)
  between operations  0.65 us (1%)
    pallas_call x1, Pallas kernels, local(): pl.pallas_call(kernel, out_shape=(jax.ShapeDtypeStruct(block, BF16), jax....  50 us
    unnamed x7, local copies, waits for them, and re-layouts  2.87 us

profile of v1, /device:TPU:7, one launch (start us, length us, event | category | flops | bytes accessed | tf_op | source)
XLA Modules:
  0.0 53.5 jit_solution(10331181623952319351)
XLA Ops:
  0.6 50.0 %shard_map.67 = (bf16[3,4,2,8,256]{4,3,2,1,0:T(8,128)(2,1)}, bf16[3,4,2,8,256]{4,3,2,1,0:T(8,128)(2,1)}, f32[2,4,256]{2,1,0:T(4,128)}) custom-call(bf16[3,4,2,8,256]{4,3,2,1,0:T(8,128)(2,1)} %vel.1, bf16[3,4,2,8,256]{4,3,2,1,0:T(8,128)(2,1)} %mag.1, bf16[3,4,2,8,256]{4,3,2,1,0:T(8,128)(2,1)} %vor.1, bf16[3,4,2,8,256]{4,3,2,1,0:T(8,128)(2,1)} %cur.1), custom_call_target="tpu_custom_call" | custom-call | tf_op jit(solution)/shard_map/pallas_call | solution.py:434
  50.6 0.0 copy-start
  50.6 1.6 %copy.10 = bf16[3,4,2,8,256]{4,3,2,1,0:T(8,128)(2,1)} copy(bf16[3,4,2,8,256]{4,3,2,1,0:T(8,128)(2,1)} %get-tuple-element.6) | data formatting | bytes 196608
  52.2 0.0 copy-done
  52.2 0.0 copy-start.1
  52.2 0.6 %copy.11 = bf16[3,4,2,8,256]{4,3,2,1,0:T(8,128)(2,1)} copy(bf16[3,4,2,8,256]{4,3,2,1,0:T(8,128)(2,1)S(1)} %copy-done) | data formatting | bytes 196608
  52.8 0.1 copy-done.1
  52.9 0.6 %copy.12 = f32[2,4,256]{2,1,0:T(4,128)} copy(f32[2,4,256]{2,1,0:T(4,128)S(1)} %copy-done.1) | data formatting | bytes 16384
Async XLA Ops:
  50.6 1.6 %copy-start = (bf16[3,4,2,8,256]{4,3,2,1,0:T(8,128)(2,1)S(1)}, bf16[3,4,2,8,256]{4,3,2,1,0:T(8,128)(2,1)}, u32[]{:S(2)}) copy-start(bf16[3,4,2,8,256]{4,3,2,1,0:T(8,128)(2,1)} %get-tuple-element.7) | copy-start | bytes 294916
  52.2 0.7 %copy-start.1 = (f32[2,4,256]{2,1,0:T(4,128)S(1)}, f32[2,4,256]{2,1,0:T(4,128)}, u32[]{:S(2)}) copy-start(f32[2,4,256]{2,1,0:T(4,128)} %get-tuple-element.8) | copy-start | bytes 24580

commit v2 on v1

--- a/solution.py
+++ b/solution.py
@@ -14,6 +14,7 @@
 HARM = 32
 RAD = 16
 NPHI = 768
+GROUP = 4
 CROW = 64
 
 
@@ -90,9 +91,10 @@
 def kernel(
     vel, mag, vor, cur,
     adv, grad, energy,
+    fields,
     tab, qt, coef, rhs, synth, wire, modes, trig, turned, grid, prod, spec, back, backf,
-    zed, out, ind, low, high, esrc, erecv, ered, efin,
-    mode_send, mode_recv, spec_send, spec_recv, halo_send, halo_recv, e_send, e_recv,
+    acc, out, ind, low, high, esrc, erecv, ered, efin,
+    field_sem, mode_send, mode_recv, spec_send, spec_recv, halo_send, halo_recv, e_send, e_recv,
 ):
     me = lax.axis_index("harm")
     my_rad = lax.axis_index("rad")
@@ -112,20 +114,28 @@
     pl.semaphore_signal(barrier, inc=1, device_id={"rad": up})
     pl.semaphore_signal(barrier, inc=1, device_id={"rad": down})
 
+    arrivals = [
+        pltpu.make_async_copy(ref, fields.at[a], field_sem.at[a])
+        for a, ref in enumerate((vel, mag, vor, cur))
+    ]
+    for arrival in arrivals:
+        arrival.start()
+
+    legendre_steps(me, tab)
+
     coef[:, 0:CROW, :] = jnp.zeros((2, CROW, 128), F32)
     coef[:, CROW + 768:, :] = jnp.zeros((2, CROW, 128), F32)
-    for a, ref in enumerate((vel, mag, vor, cur)):
+    for a, arrival in enumerate(arrivals):
+        arrival.wait()
         for half in range(2):
             lanes = pl.ds(half * 128, 128)
             coef[half, CROW + 192 * a:CROW + 192 * (a + 1), :] = (
-                ref[:, :, :, :, lanes].astype(F32).reshape(192, 128)
+                fields[a, :, :, :, :, lanes].astype(F32).reshape(192, 128)
             )
 
-    legendre_steps(me, tab)
-
     row8 = iota((8, 128), 0)
 
-    def synthesis(m, carry):
+    def synthesis(m, slot):
         for jt, rows in ((0, 128), (1, 64)):
             table = tab[jt, pl.ds(m, L, stride=8), :]
             qt[m, jt * 128:jt * 128 + rows, :] = table.T[0:rows].astype(BF16)
@@ -141,22 +151,26 @@
                         for gn, part in ((0, jnp.where(row8 < 4, rows, 0.0)),
                                          (1, jnp.where(row8 >= 4, before, 0.0))):
                             lane = gn * 256 + half * 128
-                            rhs[base:base + 16, lane:lane + 128] = jnp.concatenate(
+                            rhs[slot, base:base + 16, lane:lane + 128] = jnp.concatenate(
                                 [part, part * sgn], axis=0
                             ).astype(BF16)
                     before = rows
         lhs = jnp.concatenate([qt[m, 0:96, :], qt[m, 96:192, :]], axis=1)
         made = lax.dot_general(
-            lhs, rhs[...], (((1,), (1,)), ((), ())), preferred_element_type=F32
+            lhs, rhs[slot], (((1,), (1,)), ((), ())), preferred_element_type=F32
         ) * (1.0 / L)
         for k in range(3):
             for lt in range(3):
                 synth[k, lt, pl.ds(m, 32, stride=8), :] = made[
                     k * 32:(k + 1) * 32, lt * 128:(lt + 1) * 128
                 ]
+
+    def synthesis_group(group, carry):
+        for inner in range(GROUP):
+            synthesis(group * GROUP + inner, inner)
         return carry
 
-    lax.fori_loop(0, 8, synthesis, 0)
+    lax.fori_loop(0, 8 // GROUP, synthesis_group, 0)
     wire[...] = synth[...].astype(BF16)
 
     pl.semaphore_wait(barrier, HARM + 1)
@@ -256,32 +270,38 @@
             for c in range(6):
                 value = cross(u, w, c) + cross(j, b, c) if c < 3 else cross(u, b, c - 3)
                 value = value.astype(BF16)
-                ends = (96, ) if c < 2 else (128 - 32, 192 - 32)
-                prod[c * 16:(c + 1) * 16, cols] = value
-                for end in ends:
-                    prod[end + c * 16:end + (c + 1) * 16, cols] = value
-
-    even = iota((256, 1), 0)
-    mode_weight = jnp.where(even == 0, 1.0, 2.0)
-    wide_lane = iota((1, 128), 1)
+                base = 96 + c * 16 if c < 3 else (c - 3) * 16
+                for at in (base, base + 48):
+                    prod[at:at + 16, cols] = value
+                    if at >= 128:
+                        prod[at + 64:at + 80, cols] = value
+
+    mode_weight = jnp.where(iota((256, 1), 0) == 0, 1.0, 2.0)
+    near = iota((1, 128), 1)
+    take_cosine = (
+        (near < 48) | (near >= 96),
+        (near & 63) < 16,
+    )
 
     def analysed(k):
-        cosine = lax.dot_general(
-            trig[0], prod[0:128], (((1,), (1,)), ((), ())), preferred_element_type=F32
-        )
-        sine = lax.dot_general(
-            trig[1], prod[...], (((1,), (1,)), ((), ())), preferred_element_type=F32
+        cosine, sine = (
+            lax.dot_general(
+                trig[r], prod[...], (((1,), (1,)), ((), ())), preferred_element_type=F32
+            )
+            for r in range(2)
         )
         scale = mode_weight * factors[k]
-        first = jnp.where(wide_lane < 96, cosine, sine[:, 0:128]) * scale
-        second = sine[:, 128:256] * scale
-        return first.astype(BF16), second
+        return [
+            jnp.where(take_cosine[t], cosine[:, t * 128:t * 128 + 128], sine[:, t * 128:t * 128 + 128])
+            * scale
+            for t in range(2)
+        ]
 
     def wait_modes(k):
         pltpu.make_async_copy(modes.at[k], modes.at[k], mode_recv.at[k]).wait()
 
-    def spec_copy(part, tiles, i):
-        to = peer(i)
+    def spec_copy(part, i):
+        to, tiles = peer(i), parts[part]
         return pltpu.make_async_remote_copy(
             src_ref=spec.at[tiles, rows_of(to), :],
             dst_ref=back.at[tiles, rows_of(me), :],
@@ -290,9 +310,11 @@
             device_id={"harm": to},
         )
 
-    def send_spectra(part, tiles):
+    def send_spectra(part):
+        tiles = parts[part]
+
         def one(i, carry):
-            spec_copy(part, tiles, i).start()
+            spec_copy(part, i).start()
             return carry
 
         lax.fori_loop(1, HARM, one, 0)
@@ -300,18 +322,17 @@
             spec.at[tiles, rows_of(me), :], back.at[tiles, rows_of(me), :], spec_recv.at[part]
         ).start()
 
-    tiles_a, tiles_b = pl.ds(0, 3), pl.ds(3, 2)
+    parts = (pl.ds(0, 2), pl.ds(2, 1), pl.ds(3, 2))
     wait_modes(0)
     grid_of(0)
-    first, second0 = analysed(0)
-    spec[0] = first
-    spec[1] = second0.astype(BF16)
+    lead, trail0 = analysed(0)
+    spec[0] = lead.astype(BF16)
     wait_modes(1)
     grid_of(1)
-    first, second1 = analysed(1)
-    spec[2] = first
-    spec[1] = jnp.where(wide_lane < 64, spec[1].astype(F32), second1).astype(BF16)
-    send_spectra(0, tiles_a)
+    lead, trail1 = analysed(1)
+    spec[1] = lead.astype(BF16)
+    send_spectra(0)
+    spec[3] = jnp.where(near < 64, trail0, trail1).astype(BF16)
 
     pltpu.make_async_copy(erecv, erecv, e_recv.at[0]).wait()
     ered[...] = jnp.sum(erecv[...], axis=0, keepdims=True)
@@ -336,52 +357,58 @@
 
     wait_modes(2)
     grid_of(2)
-    first, second2 = analysed(2)
-    spec[3] = first
-    spec[4] = second2.astype(BF16)
-    send_spectra(1, tiles_b)
-
-    def wait_spectra(part, tiles):
+    lead, trail = analysed(2)
+    spec[2] = lead.astype(BF16)
+    send_spectra(1)
+    spec[4] = trail.astype(BF16)
+    send_spectra(2)
+
+    def wait_spectra(part):
+        tiles = parts[part]
         pltpu.make_async_copy(back.at[tiles], back.at[tiles], spec_recv.at[part]).wait()
-
-    wait_spectra(0, tiles_a)
-    backf[0:3] = back[0:3].astype(F32)
-    wait_spectra(1, tiles_b)
-    backf[3:5] = back[3:5].astype(F32)
+        backf[tiles] = back[tiles].astype(F32)
 
     lane_row = iota((32, 128), 1)
     gn_of = (lane_row >> 2) & 1
 
-    def latitude(m, carry):
-        tiles = [backf[t, pl.ds(m, 32, stride=8), :] for t in range(5)]
-        middle = (
-            jnp.where(lane_row < 64, tiles[1], 0.0),
-            jnp.where(lane_row >= 64, tiles[1], 0.0),
-            jnp.where(lane_row < 64, tiles[4], 0.0),
-        )
-        lead = (tiles[0], tiles[2], tiles[3])
-        for gn in range(2):
-            for k in range(3):
-                at = (gn * 3 + k) * 32
-                zed[at:at + 32, 0:128] = jnp.where(gn_of == gn, lead[k], 0.0).astype(BF16)
-                zed[at:at + 32, 128:256] = jnp.where(gn_of == gn, middle[k], 0.0).astype(BF16)
-        sums = lax.dot_general(
-            zed[...], qt[m], (((0,), (0,)), ((), ())), preferred_element_type=F32
-        )
-        sums = jnp.concatenate([sums[0:128], sums[128:192] + sums[192:256]], axis=0)
+    def split(rows):
+        return jnp.concatenate(
+            [jnp.where(gn_of == gn, part, 0.0) for gn in range(2) for part in rows], axis=0
+        ).astype(BF16)
+
+    def column(tile, m):
+        return backf[tile, pl.ds(m, 32, stride=8), :]
+
+    def table(m, ks):
+        return jnp.concatenate(
+            [qt[m, gn * 96 + ks[0] * 32:gn * 96 + ks[-1] * 32 + 32, :] for gn in range(2)], axis=0
+        )
+
+    def over_rows(values, m, ks):
+        return lax.dot_general(
+            split(values), table(m, ks), (((0,), (0,)), ((), ())), preferred_element_type=F32
+        )
+
+    def store(sums, at, kind, r, c, m):
         sign = parity_sign(m)
+        both = sums[at:at + 8] + sums[at + 8:at + 16] * sign
+        both = both[0:4] + both[4:8]
+        for half in range(2):
+            out[half, pl.ds(kind * 192 + c * 64 + r * 8 + m, 4, stride=16), :] = both[
+                :, half * 128:(half + 1) * 128
+            ]
+
+    wait_spectra(0)
+    for m in range(8):
+        acc[m] = over_rows([column(0, m), column(1, m)], m, (0, 1))
+    wait_spectra(1)
+    for m in range(8):
+        sums = acc[m] + over_rows([column(2, m)], m, (2,))
         for r in range(2):
-            for c in range(6):
-                base = r * 96 + c * 16
-                both = sums[base:base + 8] + sums[base + 8:base + 16] * sign
-                both = both[0:4] + both[4:8]
-                for half in range(2):
-                    out[half, pl.ds(c * 64 + r * 8 + m, 4, stride=16), :] = both[
-                        :, half * 128:(half + 1) * 128
-                    ]
-        return carry
-
-    lax.fori_loop(0, 8, latitude, 0)
+            for c in range(3):
+                store(sums, r * 48 + c * 16, 1, r, c, m)
+        for c in range(2):
+            store(sums, 96 + c * 16, 0, 0, c, m)
 
     for half in range(2):
         lanes = pl.ds(half * 128, 128)
@@ -398,6 +425,22 @@
     to_up.start()
     to_down.start()
 
+    wait_spectra(2)
+    for m in range(8):
+        pair, last = column(3, m), column(4, m)
+        sums = over_rows(
+            [
+                jnp.where(lane_row < 64, pair, 0.0),
+                jnp.where(lane_row >= 64, pair, 0.0),
+                jnp.where(lane_row < 64, last, 0.0),
+            ],
+            m, (0, 1, 2),
+        )
+        sums = sums[0:64] + sums[64:128]
+        store(sums, 0, 0, 0, 2, m)
+        for c in range(3):
+            store(sums, 16 + c * 16, 0, 1, c, m)
+
     for half in range(2):
         lanes = pl.ds(half * 128, 128)
         adv[:, :, :, :, lanes] = out[half, 0:192, :].reshape(3, 4, 2, 8, 128).astype(BF16)
@@ -421,8 +464,8 @@
     for k in range(3):
         sent = wire.at[k, :, others, :]
         pltpu.make_async_copy(sent, sent, mode_send.at[k]).wait()
-    for part, tiles in ((0, tiles_a), (1, tiles_b)):
-        sent = spec.at[tiles, others, :]
+    for part in range(3):
+        sent = spec.at[parts[part], others, :]
         pltpu.make_async_copy(sent, sent, spec_send.at[part]).wait()
     pltpu.make_async_copy(erecv.at[pl.ds(0, 31)], erecv.at[pl.ds(0, 31)], e_send.at[0]).wait()
     pltpu.make_async_copy(efin.at[pl.ds(0, 15)], efin.at[pl.ds(0, 15)], e_send.at[1]).wait()
@@ -438,13 +481,14 @@
             jax.ShapeDtypeStruct(block, BF16),
             jax.ShapeDtypeStruct((2, 4, L), F32),
         ),
-        in_specs=[vmem] * 4,
+        in_specs=[pl.BlockSpec(memory_space=pl.ANY)] * 4,
         out_specs=(vmem,) * 3,
         scratch_shapes=[
+            pltpu.VMEM((4,) + block, BF16),
             pltpu.VMEM((2, L * 8, 128), F32),
             pltpu.VMEM((8, 192, L), BF16),
             pltpu.VMEM((2, 768 + 2 * CROW, 128), F32),
-            pltpu.VMEM((384, 512), BF16),
+            pltpu.VMEM((GROUP, 384, 512), BF16),
             pltpu.VMEM((3, 3, 256, 128), F32),
             pltpu.VMEM((3, 3, 256, 128), BF16),
             pltpu.VMEM((3, 3, 256, 128), BF16),
@@ -455,7 +499,7 @@
             pltpu.VMEM((5, 256, 128), BF16),
             pltpu.VMEM((5, 256, 128), BF16),
             pltpu.VMEM((5, 256, 128), F32),
-            pltpu.VMEM((192, 256), BF16),
+            pltpu.VMEM((8, 128, L), F32),
             pltpu.VMEM((2, 384, 128), F32),
             pltpu.VMEM((3, 4, 2, 8, L), BF16),
             pltpu.VMEM((3, 2, 8, L), BF16),
@@ -464,10 +508,11 @@
             pltpu.VMEM((HARM, 1, 128), F32),
             pltpu.VMEM((1, 1, 128), F32),
             pltpu.VMEM((16, 1, 128), F32),
+            pltpu.SemaphoreType.DMA((4,)),
             pltpu.SemaphoreType.DMA((3,)),
             pltpu.SemaphoreType.DMA((3,)),
-            pltpu.SemaphoreType.DMA((2,)),
-            pltpu.SemaphoreType.DMA((2,)),
+            pltpu.SemaphoreType.DMA((3,)),
+            pltpu.SemaphoreType.DMA((3,)),
             pltpu.SemaphoreType.DMA((2,)),
             pltpu.SemaphoreType.DMA((2,)),
             pltpu.SemaphoreType.DMA((2,)),

time: 53.7 us -> 50.4 us (0.939)
  Pallas kernels: 50 us -> 46.7 us
    pallas_call x1, Pallas kernels: 50 us -> 46.7 us  [local(): pl.pallas_call(kernel, out_shape=(jax.ShapeDtypeStruct(block, BF16), jax....]
where the time goes in v2:
time: 50.4 us; the launch traced here: 50.2 us
  Pallas kernels  46.7 us (93%)
  local copies, waits for them, and re-layouts  2.87 us (6%)
  between operations  0.65 us (1%)
    pallas_call x1, Pallas kernels, local(): pl.pallas_call(kernel, out_shape=(jax.ShapeDtypeStruct(block, BF16), jax....  46.7 us
    unnamed x7, local copies, waits for them, and re-layouts  2.87 us

profile of v2, /device:TPU:7, one launch (start us, length us, event | category | flops | bytes accessed | tf_op | source)
XLA Modules:
  0.0 50.2 jit_solution(1687236506407825978)
XLA Ops:
  0.6 46.7 %shard_map.67 = (bf16[3,4,2,8,256]{4,3,2,1,0:T(8,128)(2,1)}, bf16[3,4,2,8,256]{4,3,2,1,0:T(8,128)(2,1)}, f32[2,4,256]{2,1,0:T(4,128)}) custom-call(bf16[3,4,2,8,256]{4,3,2,1,0:T(8,128)(2,1)} %vel.1, bf16[3,4,2,8,256]{4,3,2,1,0:T(8,128)(2,1)} %mag.1, bf16[3,4,2,8,256]{4,3,2,1,0:T(8,128)(2,1)} %vor.1, bf16[3,4,2,8,256]{4,3,2,1,0:T(8,128)(2,1)} %cur.1), custom_call_target="tpu_custom_call" | custom-call | tf_op jit(solution)/shard_map/pallas_call | solution.py:477
  47.3 0.0 copy-start
  47.3 1.6 %copy.10 = bf16[3,4,2,8,256]{4,3,2,1,0:T(8,128)(2,1)} copy(bf16[3,4,2,8,256]{4,3,2,1,0:T(8,128)(2,1)} %get-tuple-element.6) | data formatting | bytes 196608
  48.9 0.0 copy-done
  48.9 0.0 copy-start.1
  48.9 0.6 %copy.11 = bf16[3,4,2,8,256]{4,3,2,1,0:T(8,128)(2,1)} copy(bf16[3,4,2,8,256]{4,3,2,1,0:T(8,128)(2,1)S(1)} %copy-done) | data formatting | bytes 196608
  49.5 0.1 copy-done.1
  49.6 0.6 %copy.12 = f32[2,4,256]{2,1,0:T(4,128)} copy(f32[2,4,256]{2,1,0:T(4,128)S(1)} %copy-done.1) | data formatting | bytes 16384
Async XLA Ops:
  47.3 1.6 %copy-start = (bf16[3,4,2,8,256]{4,3,2,1,0:T(8,128)(2,1)S(1)}, bf16[3,4,2,8,256]{4,3,2,1,0:T(8,128)(2,1)}, u32[]{:S(2)}) copy-start(bf16[3,4,2,8,256]{4,3,2,1,0:T(8,128)(2,1)} %get-tuple-element.7) | copy-start | bytes 294916
  48.9 0.7 %copy-start.1 = (f32[2,4,256]{2,1,0:T(4,128)S(1)}, f32[2,4,256]{2,1,0:T(4,128)}, u32[]{:S(2)}) copy-start(f32[2,4,256]{2,1,0:T(4,128)} %get-tuple-element.8) | copy-start | bytes 24580

commit v3 on v2

v3 whole, which is shorter than its diff:
```python
import jax
import jax.numpy as jnp
from jax import lax
from jax.experimental import pallas as pl
from jax.experimental.pallas import tpu as pltpu
from jax.sharding import PartitionSpec as P

F32 = jnp.float32
BF16 = jnp.bfloat16
PI = 3.14159265358979
L = 256
HARM = 32
RAD = 16
NPHI = 768
GROUP = 4

PAIRS = ((0, 3), (1, 2))
EARLY = [(c, 0) for c in range(8)]
LATER = [(c, 0) for c in range(8, 12)] + [(c, 1) for c in range(12)]
SLOT_ROW = {}
for at, (c, pair) in enumerate(EARLY):
    for r in range(2):
        SLOT_ROW[c, pair, r] = r * 64 + at * 8
for at, (c, pair) in enumerate(LATER):
    for r in range(2):
        SLOT_ROW[c, pair, r] = 128 + r * 128 + at * 8
ROW_SLOT = {row: slot for slot, row in SLOT_ROW.items()}


def sin_poly(y):
    z = y * y
    s = -1.0 / 39916800.0
    for c in (1.0 / 362880.0, -1.0 / 5040.0, 1.0 / 120.0, -1.0 / 6.0, 1.0):
        s = s * z + c
    return y * s


def cos_768(q):
    return sin_poly((192.0 - jnp.minimum(q, 768.0 - q)) * (PI / 384.0))


def mod_768(v):
    return v - 768.0 * jnp.floor((v + 0.5) * (1.0 / 768.0))


def iota(shape, dim):
    return lax.broadcasted_iota(jnp.int32, shape, dim)


def fiota(shape, dim):
    return iota(shape, dim).astype(F32)


def parity_sign(order, rows=1):
    return 1.0 - 2.0 * ((iota((rows, L), 1) + order) & 1).astype(F32)


def dot_nt(a, b):
    return lax.dot_general(a, b, (((1,), (1,)), ((), ())), preferred_element_type=F32)


def dot_tn(a, b):
    return lax.dot_general(a, b, (((0,), (0,)), ((), ())), preferred_element_type=F32)


def legendre_steps(me, tab):
    order = (me * 8 + iota((8, 128), 0)).astype(F32)
    order_sq = order * order
    degree = fiota((8, L), 1)
    own = (me * 8 + iota((8, L), 0)).astype(F32)
    logs = 0.5 * jnp.log((2.0 * degree + 1.0) / jnp.maximum(2.0 * degree, 1.0))
    taken = jnp.where((degree >= 1.0) & (degree <= own), logs, 0.0)
    log_start = 0.5 * jnp.log(jnp.full((8, 1), 0.5, F32)) + jnp.sum(taken, axis=1, keepdims=True)
    cosine, sector, unscale = [], [], []
    for jt in range(2):
        odd = 2.0 * (fiota((8, 128), 1) + 128.0 * jt) + 1.0
        cosine.append(sin_poly((384.0 - odd) * (PI / 768.0)))
        sine = sin_poly(jnp.minimum(odd, 768.0 - odd) * (PI / 768.0))
        log_sector = log_start + order * jnp.log(sine)
        sector.append(jnp.exp(jnp.maximum(log_sector, -60.0)))
        unscale.append(jnp.exp(jnp.minimum(log_sector + 60.0, 0.0)))
    zero = jnp.zeros((8, 128), F32)
    per = 16

    def block(index, state):
        q0, p0, q1, p1, back = state
        for inner in range(per):
            deg_i = index * per + inner
            deg = deg_i.astype(F32)
            sq = deg * deg
            live = order < deg
            t = (4.0 * sq - 1.0) / jnp.where(live, sq - order_sq, 1.0)
            a = jnp.where(live, jnp.sqrt(t), 0.0)
            ab = a * back
            back = jnp.where(live, lax.rsqrt(t), 0.0)
            start = order == deg
            n0 = a * cosine[0] * q0 + (jnp.where(start, sector[0], 0.0) - ab * p0)
            n1 = a * cosine[1] * q1 + (jnp.where(start, sector[1], 0.0) - ab * p1)
            row = pl.ds(pl.multiple_of(deg_i * 8, 8), 8)
            tab[0, row, :] = n0 * unscale[0]
            tab[1, row, :] = n1 * unscale[1]
            q0, p0, q1, p1 = n0, q0, n1, q1
        return q0, p0, q1, p1, back

    lax.fori_loop(0, L // per, block, (zero, zero, zero, zero, zero))


def kernel(
    vel, mag, vor, cur,
    adv, grad, energy,
    fields,
    tab, qt, coef, rhs, synth, wire, modes, trig, turned, turned_early, grid, grid_early,
    prod, prod_early, spec, back, backf,
    acc, out, ind, low, high, esrc, erecv, ered, efin,
    field_sem, mode_send, mode_recv, spec_send, spec_recv, halo_send, halo_recv, e_send, e_recv,
):
    me = lax.axis_index("harm")
    my_rad = lax.axis_index("rad")
    above = my_rad < RAD - 1
    below = my_rad > 0

    def peer(i):
        return lax.rem(me + i, HARM)

    barrier = pltpu.get_barrier_semaphore()

    def greet(i, carry):
        pl.semaphore_signal(barrier, inc=1, device_id={"harm": peer(i)})
        return carry

    lax.fori_loop(1, HARM, greet, 0)

    @pl.when(above)
    def _():
        pl.semaphore_signal(barrier, inc=1, device_id={"rad": my_rad + 1})

    @pl.when(below)
    def _():
        pl.semaphore_signal(barrier, inc=1, device_id={"rad": my_rad - 1})

    arrivals = [
        pltpu.make_async_copy(ref, fields.at[a], field_sem.at[a])
        for a, ref in enumerate((vel, mag, vor, cur))
    ]
    for arrival in arrivals:
        arrival.start()

    @pl.when(jnp.logical_not(below))
    def _():
        low[...] = jnp.zeros(low.shape, BF16)

    @pl.when(jnp.logical_not(above))
    def _():
        high[...] = jnp.zeros(high.shape, BF16)

    legendre_steps(me, tab)

    for a, arrival in enumerate(arrivals):
        arrival.wait()
        for c in range(3):
            for r in range(2):
                for pair in range(2):
                    both = fields[a, c, PAIRS[pair][0], r], fields[a, c, PAIRS[pair][1], r]
                    both = jnp.concatenate([v.astype(F32) for v in both], axis=0)
                    at = ((r * 12 + a * 3 + c) * 2 + pair) * 64
                    for half in range(2):
                        part = both[:, half * 128:(half + 1) * 128]
                        for copy in range(4):
                            coef[half, at + copy * 16:at + copy * 16 + 16, :] = part

    slot_row = iota((8, 128), 0)

    def synthesis(m, slot):
        for jt, rows in ((0, 128), (1, 64)):
            table = tab[jt, pl.ds(m, L, stride=8), :]
            qt[m, jt * 128:jt * 128 + rows, :] = table.T[0:rows].astype(BF16)
        sign = parity_sign(m, 8)
        for half in range(2):
            sgn = jnp.where(slot_row >= 4, sign[:, half * 128:(half + 1) * 128], 1.0)
            keep = [jnp.where(((slot_row >> 1) & 1) == gn, sgn, 0.0) for gn in range(2)]
            for row in range(0, 384, 16):
                values = []
                for at in (row, row + 8):
                    c, pair, r = ROW_SLOT[at]
                    first = ((r * 12 + c) * 2 + pair) * 64
                    values.append(coef[half, pl.ds(first + m, 8, stride=8), :])
                for gn in range(2):
                    lane = gn * 256 + half * 128
                    rhs[slot, row:row + 16, lane:lane + 128] = jnp.concatenate(
                        [v * keep[gn] for v in values], axis=0
                    ).astype(BF16)
        lhs = jnp.concatenate([qt[m, 0:96, :], qt[m, 96:192, :]], axis=1)
        made = dot_nt(lhs, rhs[slot]) * (1.0 / L)
        for k in range(3):
            for lt in range(3):
                synth[k, lt, pl.ds(m, 32, stride=8), :] = made[
                    k * 32:(k + 1) * 32, lt * 128:(lt + 1) * 128
                ]

    def synthesis_group(group, carry):
        for inner in range(GROUP):
            synthesis(group * GROUP + inner, inner)
        return carry

    lax.fori_loop(0, 8 // GROUP, synthesis_group, 0)
    wire[...] = synth[...].astype(BF16)

    pl.semaphore_wait(barrier, HARM - 1 + above.astype(jnp.int32) + below.astype(jnp.int32))

    def rows_of(device):
        return pl.ds(pl.multiple_of(device * 8, 8), 8)

    def mode_part(ref, group, rows):
        if group == 0:
            return ref.at[:, 0, rows, :]
        return ref.at[group - 1, pl.ds(1, 2), rows, :]

    def send_modes(group):
        def one(i, carry):
            to = peer(i)
            pltpu.make_async_remote_copy(
                src_ref=mode_part(wire, group, rows_of(to)),
                dst_ref=mode_part(modes, group, rows_of(me)),
                send_sem=mode_send.at[group],
                recv_sem=mode_recv.at[group],
                device_id={"harm": to},
            ).start()
            return carry

        lax.fori_loop(1, HARM, one, 0)
        pltpu.make_async_copy(
            mode_part(wire, group, rows_of(me)),
            mode_part(modes, group, rows_of(me)),
            mode_recv.at[group],
        ).start()

    def wait_modes(group):
        landed = mode_part(modes, group, pl.ds(0, 256))
        pltpu.make_async_copy(landed, landed, mode_recv.at[group]).wait()

    send_modes(0)
    send_modes(1)

    order8 = me * 8 + iota((8, 128), 0)
    for half in range(2):
        degree = iota((8, 128), 1) + 128 * half
        weight = jnp.where(degree >= order8, 1.0 / (2.0 * degree.astype(F32) + 1.0), 0.0)
        weights = (
            weight * jnp.where(order8 == 0, 0.5, 1.0),
            weight * jnp.where(order8 == 0, 0.0, 1.0),
        )
        for q in range(2):
            for s in range(4):
                pair = 0 if s in PAIRS[0] else 1
                total = jnp.zeros((8, 128), F32)
                for c in range(3):
                    for r in range(2):
                        at = ((r * 12 + q * 3 + c) * 2 + pair) * 64 + PAIRS[pair].index(s) * 8
                        value = coef[half, at:at + 8, :]
                        total += value * value * weights[r]
                esrc[(q * 4 + s) * 2 + half] = jnp.sum(total, axis=0, keepdims=True)

    def send_energy(i, carry):
        to = peer(i)
        pltpu.make_async_remote_copy(
            src_ref=esrc.at[lax.rem(to, 16)],
            dst_ref=erecv.at[me],
            send_sem=e_send.at[0],
            recv_sem=e_recv.at[0],
            device_id={"harm": to},
        ).start()
        return carry

    lax.fori_loop(1, HARM, send_energy, 0)
    pltpu.make_async_copy(esrc.at[lax.rem(me, 16)], erecv.at[me], e_recv.at[0]).start()

    def trig_rows(b, carry):
        angle = mod_768((b * 8 + iota((8, NPHI), 0)).astype(F32) * fiota((8, NPHI), 1))
        rows = pl.ds(pl.multiple_of(b * 8, 8), 8)
        trig[0, rows, :] = cos_768(angle).astype(BF16)
        trig[1, rows, :] = cos_768(jnp.where(angle >= 192.0, angle - 192.0, angle + 576.0)).astype(BF16)
        return carry

    lax.fori_loop(0, 32, trig_rows, 0)

    lane = iota((1, 128), 1)
    factors = []
    for k in range(3):
        row = ((lane >> 1) & 1) * 96 + k * 32 + me
        wave = fiota((192, 128), 0) + 1.0
        odd = (2 * row + 1).astype(F32)
        series = cos_768(mod_768(wave * odd)) / (4.0 * wave * wave - 1.0)
        weight = (2.0 / 384.0) * (1.0 - 2.0 * jnp.sum(series, axis=0, keepdims=True))
        factors.append(weight * (256.0 / 768.0))
    mixed = jnp.where(lane < 32, factors[0], jnp.where(lane < 64, factors[1], factors[2]))
    mode_weight = jnp.where(iota((256, 1), 0) == 0, 1.0, 2.0)
    prod[:, 128:256, :] = jnp.zeros((3, 128, NPHI), BF16)
    prod_early[96:128, :] = jnp.zeros((32, NPHI), BF16)

    def cross(x, y, i):
        n, o = (i + 1) % 3, (i + 2) % 3
        return x[n] * y[o] - x[o] * y[n]

    def rounded_pair(first, second):
        return jnp.concatenate([first, second], axis=0).astype(BF16)

    def send_spectra(group):
        def one(i, carry):
            to = peer(i)
            pltpu.make_async_remote_copy(
                src_ref=spec.at[group, rows_of(to), :],
                dst_ref=back.at[group, rows_of(me), :],
                send_sem=spec_send.at[group],
                recv_sem=spec_recv.at[group],
                device_id={"harm": to},
            ).start()
            return carry

        lax.fori_loop(1, HARM, one, 0)
        pltpu.make_async_copy(
            spec.at[group, rows_of(me), :], back.at[group, rows_of(me), :], spec_recv.at[group]
        ).start()

    def wait_spectra(group):
        pltpu.make_async_copy(back.at[group], back.at[group], spec_recv.at[group]).wait()
        backf[group] = back[group].astype(F32)

    wait_modes(0)
    for k in range(3):
        turned_early[k] = modes[k, 0].T
    grid_early[...] = sum(
        jnp.dot(
            jnp.concatenate([turned_early[k, r * 64:(r + 1) * 64] for k in range(3)], axis=0),
            trig[r], preferred_element_type=F32,
        )
        for r in range(2)
    )
    even_row = (iota((8, 128), 0) & 1) == 0
    for k in range(3):
        for pt in range(6):
            cols = slice(pt * 128, (pt + 1) * 128)
            g = [grid_early[k * 64 + c * 8:k * 64 + c * 8 + 8, cols] for c in range(6)]
            x, y, z = (cross(g[0:3], g[3:6], i) for i in range(3))
            lower = jnp.where(even_row, x, pltpu.roll(y, 1, 0))
            upper = jnp.where(even_row, pltpu.roll(x, 7, 0), y).astype(BF16)
            pair = rounded_pair(lower, z)
            for r in range(2):
                prod_early[k * 32 + r * 16:k * 32 + r * 16 + 16, cols] = pair
                prod[k, r * 32:r * 32 + 8, cols] = upper
    early_c, early_s = (dot_nt(trig[r], prod_early[...]) for r in range(2))
    spec[0] = (
        jnp.where(((lane >> 4) & 1) == 0, early_c, early_s) * (mode_weight * mixed)
    ).astype(BF16)
    send_spectra(0)
    send_modes(2)
    send_modes(3)

    def later(k):
        for lt in range(2):
            turned[lt * 128:(lt + 1) * 128, :] = modes[k, 1 + lt].T
        grid[...] = sum(
            jnp.dot(turned[r * 128:(r + 1) * 128], trig[r], preferred_element_type=F32)
            for r in range(2)
        )
        for pt in range(6):
            cols = slice(pt * 128, (pt + 1) * 128)

            def value(c, pair):
                if pair == 0 and c < 8:
                    return grid_early[k * 64 + c * 8:k * 64 + c * 8 + 8, cols]
                at = (c - 8) * 8 if pair == 0 else 32 + c * 8
                return grid[at:at + 8, cols]

            u, b, w, j = ([value(v * 3 + i, 1) for i in range(3)] for v in range(4))
            inner = [cross(u, w, i) + cross(j, b, i) for i in range(3)]
            curl = [cross(u, b, i) for i in range(3)]
            u, b, w, j = ([value(v * 3 + i, 0) for i in range(3)] for v in range(4))
            ends = [cross(u, w, i) + cross(j, b, i) for i in range(3)]
            for r in range(2):
                prod[k, r * 32 + 8:r * 32 + 16, cols] = curl[0].astype(BF16)
                prod[k, r * 32 + 16:r * 32 + 32, cols] = rounded_pair(curl[1], curl[2])
                prod[k, 64 + r * 32:64 + r * 32 + 16, cols] = rounded_pair(ends[0], ends[1])
                prod[k, 80 + r * 32:80 + r * 32 + 16, cols] = rounded_pair(ends[2], inner[0])
                at = 128 + 32 * k + 16 * r
                prod[k, at:at + 16, cols] = rounded_pair(inner[1], inner[2])
        cosine, sine = (dot_nt(trig[r], prod[k]) for r in range(2))
        scale = mode_weight * factors[k]
        lead = jnp.where(((lane >> 5) & 1) == 0, cosine[:, 0:128], sine[:, 0:128]) * scale
        trail = jnp.where(((lane >> 4) & 1) == 0, cosine[:, 128:256], sine[:, 128:256]) * scale
        spec[1 + k] = lead.astype(BF16)
        return trail

    wait_modes(1)
    trail = later(0)
    send_spectra(1)

    col = iota((32, 128), 1)
    col_gn = (col >> 1) & 1

    def column(tile, m):
        return backf[tile, pl.ds(m, 32, stride=8), :]

    def table(m, ks):
        return jnp.concatenate(
            [qt[m, gn * 96 + ks[0] * 32:gn * 96 + ks[-1] * 32 + 32, :] for gn in range(2)], axis=0
        )

    def over_rows(values, m, ks):
        kept = jnp.concatenate(
            [jnp.where(col_gn == gn, part, 0.0) for gn in range(2) for part in values], axis=0
        ).astype(BF16)
        return dot_tn(kept, table(m, ks))

    def over_mixed(tile, m):
        values = column(tile, m)
        sums = over_rows(
            [jnp.where((col >> 5) == k, values, 0.0) for k in range(3)], m, (0, 1, 2)
        )
        return sums[0:32] + sums[32:64] + sums[64:96]

    lower_half = iota((8, L), 0) < 4

    def store(sums, at, row, stride, m):
        v = sums[at:at + 8] * jnp.where(lower_half, 1.0, parity_sign(m, 8))
        v = v + pltpu.roll(v, 4, 0)
        v = v + pltpu.roll(v, 6, 0)
        for half in range(2):
            out[half, pl.ds(row + m, 2, stride=stride), :] = v[0:2, half * 128:(half + 1) * 128]

    def keep_induction(s):
        for c in range(3):
            for half in range(2):
                rows = 192 + c * 64 + s * 16
                lanes = pl.ds(half * 128, 128)
                ind[c, s, :, :, lanes] = out[half, rows:rows + 16, :].reshape(2, 8, 128).astype(BF16)

    def halo_down():
        return pltpu.make_async_remote_copy(
            src_ref=ind.at[:, 0], dst_ref=high, send_sem=halo_send.at[1], recv_sem=halo_recv.at[1],
            device_id={"rad": my_rad - 1},
        )

    def halo_up():
        return pltpu.make_async_remote_copy(
            src_ref=ind.at[:, 3], dst_ref=low, send_sem=halo_send.at[0], recv_sem=halo_recv.at[0],
            device_id={"rad": my_rad + 1},
        )

    wait_spectra(0)
    for m in range(8):
        sums = over_mixed(0, m)
        for r in range(2):
            store(sums, r * 16, 192 + r * 8, 64, m)
            store(sums, r * 16 + 8, 192 + 128 + r * 8, 48, m)
    keep_induction(0)

    @pl.when(below)
    def _():
        halo_down().start()

    wait_modes(2)
    trail = jnp.where((lane >> 5) == 1, later(1), trail)
    send_spectra(2)

    pltpu.make_async_copy(erecv, erecv, e_recv.at[0]).wait()
    ered[...] = jnp.sum(erecv[...], axis=0, keepdims=True)
    mine = lax.rem(me, 16)

    def send_row(i, carry):
        pltpu.make_async_remote_copy(
            src_ref=ered.at[0],
            dst_ref=efin.at[mine],
            send_sem=e_send.at[1],
            recv_sem=e_recv.at[1],
            device_id={"harm": me - mine + lax.rem(mine + i, 16)},
        ).start()
        return carry

    lax.fori_loop(1, 16, send_row, 0)
    pltpu.make_async_copy(ered.at[0], efin.at[mine], e_recv.at[1]).start()

    wait_modes(3)
    trail = jnp.where((lane >> 5) == 2, later(2), trail)
    send_spectra(3)
    spec[4] = trail.astype(BF16)
    send_spectra(4)

    wait_spectra(1)
    wait_spectra(2)
    for m in range(8):
        acc[m] = over_rows([column(1, m), column(2, m)], m, (0, 1))
    wait_spectra(3)
    for m in range(8):
        sums = acc[m] + over_rows([column(3, m)], m, (2,))
        for r in range(2):
            store(sums, r * 32, 192 + 48 + r * 8, 64, m)
            for c in range(3):
                store(sums, r * 32 + 8 + c * 8, 192 + c * 64 + 16 + r * 8, 16, m)
                store(sums, 64 + r * 32 + c * 8, c * 64 + r * 8, 48, m)
            store(sums, 64 + r * 32 + 24, 16 + r * 8, 16, m)
    keep_induction(3)

    @pl.when(above)
    def _():
        halo_up().start()

    keep_induction(1)
    keep_induction(2)

    wait_spectra(4)
    for m in range(8):
        sums = over_mixed(4, m)
        for r in range(2):
            for c in (1, 2):
                store(sums, r * 16 + (c - 1) * 8, c * 64 + 16 + r * 8, 16, m)

    for half in range(2):
        lanes = pl.ds(half * 128, 128)
        adv[:, :, :, :, lanes] = out[half, 0:192, :].reshape(3, 4, 2, 8, 128).astype(BF16)
    pltpu.make_async_copy(efin, efin, e_recv.at[1]).wait()
    for q in range(2):
        for s in range(4):
            for half in range(2):
                energy[q, s:s + 1, half * 128:(half + 1) * 128] = efin[(q * 4 + s) * 2 + half]

    shells = [ind[:, s].astype(F32) for s in range(4)]
    grad[:, 1] = ((shells[2] - shells[0]) * 0.5).astype(BF16)
    grad[:, 2] = ((shells[3] - shells[1]) * 0.5).astype(BF16)

    @pl.when(below)
    def _():
        halo_down().wait_send()
        halo_up().wait_recv()

    grad[:, 0] = ((shells[1] - low[...].astype(F32)) * 0.5).astype(BF16)

    @pl.when(above)
    def _():
        halo_up().wait_send()
        halo_down().wait_recv()

    grad[:, 3] = ((high[...].astype(F32) - shells[2]) * 0.5).astype(BF16)

    others = pl.ds(0, (HARM - 1) * 8)
    for group in range(4):
        sent = mode_part(wire, group, others)
        pltpu.make_async_copy(sent, sent, mode_send.at[group]).wait()
    for group in range(5):
        sent = spec.at[group, others, :]
        pltpu.make_async_copy(sent, sent, spec_send.at[group]).wait()
    pltpu.make_async_copy(erecv.at[pl.ds(0, 31)], erecv.at[pl.ds(0, 31)], e_send.at[0]).wait()
    pltpu.make_async_copy(efin.at[pl.ds(0, 15)], efin.at[pl.ds(0, 15)], e_send.at[1]).wait()


def local(velocity, magnetic, vorticity, current):
    vmem = pl.BlockSpec(memory_space=pltpu.VMEM)
    block = velocity.shape
    return pl.pallas_call(
        kernel,
        out_shape=(
            jax.ShapeDtypeStruct(block, BF16),
            jax.ShapeDtypeStruct(block, BF16),
            jax.ShapeDtypeStruct((2, 4, L), F32),
        ),
        in_specs=[pl.BlockSpec(memory_space=pl.ANY)] * 4,
        out_specs=(vmem,) * 3,
        scratch_shapes=[
            pltpu.VMEM((4,) + block, BF16),
            pltpu.VMEM((2, L * 8, 128), F32),
            pltpu.VMEM((8, 192, L), BF16),
            pltpu.VMEM((2, 48 * 64, 128), F32),
            pltpu.VMEM((GROUP, 384, 512), BF16),
            pltpu.VMEM((3, 3, 256, 128), F32),
            pltpu.VMEM((3, 3, 256, 128), BF16),
            pltpu.VMEM((3, 3, 256, 128), BF16),
            pltpu.VMEM((2, 256, NPHI), BF16),
            pltpu.VMEM((256, 256), BF16),
            pltpu.VMEM((3, 128, 256), BF16),
            pltpu.VMEM((128, NPHI), F32),
            pltpu.VMEM((192, NPHI), F32),
            pltpu.VMEM((3, 256, NPHI), BF16),
            pltpu.VMEM((128, NPHI), BF16),
            pltpu.VMEM((5, 256, 128), BF16),
            pltpu.VMEM((5, 256, 128), BF16),
            pltpu.VMEM((5, 256, 128), F32),
            pltpu.VMEM((8, 128, L), F32),
            pltpu.VMEM((2, 384, 128), F32),
            pltpu.VMEM((3, 4, 2, 8, L), BF16),
            pltpu.VMEM((3, 2, 8, L), BF16),
            pltpu.VMEM((3, 2, 8, L), BF16),
            pltpu.VMEM((16, 1, 128), F32),
            pltpu.VMEM((HARM, 1, 128), F32),
            pltpu.VMEM((1, 1, 128), F32),
            pltpu.VMEM((16, 1, 128), F32),
            pltpu.SemaphoreType.DMA((4,)),
            pltpu.SemaphoreType.DMA((4,)),
            pltpu.SemaphoreType.DMA((4,)),
            pltpu.SemaphoreType.DMA((5,)),
            pltpu.SemaphoreType.DMA((5,)),
            pltpu.SemaphoreType.DMA((2,)),
            pltpu.SemaphoreType.DMA((2,)),
            pltpu.SemaphoreType.DMA((2,)),
            pltpu.SemaphoreType.DMA((2,)),
        ],
        compiler_params=pltpu.CompilerParams(collective_id=0, has_side_effects=True),
    )(velocity, magnetic, vorticity, current)


def solution(mesh):
    split = P(None, "rad", None, "harm", None)
    return jax.shard_map(
        local,
        mesh=mesh,
        in_specs=(split,) * 4,
        out_specs=(split, split, P(None, "rad", None)),
        check_vma=False,
    )
```

time: 50.4 us -> 47.2 us (0.937)
  Pallas kernels: 46.7 us -> 43.2 us
    pallas_call x1, Pallas kernels: 46.7 us -> 43.2 us  [local(): pl.pallas_call(kernel, out_shape=(jax.ShapeDtypeStruct(block, BF16), jax....]
where the time goes in v3:
time: 47.2 us; the launch traced here: 46.7 us
  Pallas kernels  43.2 us (92%)
  local copies, waits for them, and re-layouts  2.87 us (6%)
  between operations  0.65 us (1%)
    pallas_call x1, Pallas kernels, local(): pl.pallas_call(kernel, out_shape=(jax.ShapeDtypeStruct(block, BF16), jax....  43.2 us
    unnamed x7, local copies, waits for them, and re-layouts  2.87 us

profile of v3, /device:TPU:7, one launch (start us, length us, event | category | flops | bytes accessed | tf_op | source)
XLA Modules:
  0.0 46.7 jit_solution(5871917207470983773)
XLA Ops:
  0.6 43.2 %shard_map.67 = (bf16[3,4,2,8,256]{4,3,2,1,0:T(8,128)(2,1)}, bf16[3,4,2,8,256]{4,3,2,1,0:T(8,128)(2,1)}, f32[2,4,256]{2,1,0:T(4,128)}) custom-call(bf16[3,4,2,8,256]{4,3,2,1,0:T(8,128)(2,1)} %vel.1, bf16[3,4,2,8,256]{4,3,2,1,0:T(8,128)(2,1)} %mag.1, bf16[3,4,2,8,256]{4,3,2,1,0:T(8,128)(2,1)} %vor.1, bf16[3,4,2,8,256]{4,3,2,1,0:T(8,128)(2,1)} %cur.1), custom_call_target="tpu_custom_call" | custom-call | tf_op jit(solution)/shard_map/pallas_call | solution.py:558
  43.8 0.0 copy-start
  43.8 1.6 %copy.10 = bf16[3,4,2,8,256]{4,3,2,1,0:T(8,128)(2,1)} copy(bf16[3,4,2,8,256]{4,3,2,1,0:T(8,128)(2,1)} %get-tuple-element.6) | data formatting | bytes 196608
  45.4 0.0 copy-done
  45.4 0.0 copy-start.1
  45.4 0.6 %copy.11 = bf16[3,4,2,8,256]{4,3,2,1,0:T(8,128)(2,1)} copy(bf16[3,4,2,8,256]{4,3,2,1,0:T(8,128)(2,1)S(1)} %copy-done) | data formatting | bytes 196608
  46.0 0.1 copy-done.1
  46.1 0.6 %copy.12 = f32[2,4,256]{2,1,0:T(4,128)} copy(f32[2,4,256]{2,1,0:T(4,128)S(1)} %copy-done.1) | data formatting | bytes 16384
Async XLA Ops:
  43.8 1.6 %copy-start = (bf16[3,4,2,8,256]{4,3,2,1,0:T(8,128)(2,1)S(1)}, bf16[3,4,2,8,256]{4,3,2,1,0:T(8,128)(2,1)}, u32[]{:S(2)}) copy-start(bf16[3,4,2,8,256]{4,3,2,1,0:T(8,128)(2,1)} %get-tuple-element.7) | copy-start | bytes 294916
  45.4 0.7 %copy-start.1 = (f32[2,4,256]{2,1,0:T(4,128)S(1)}, f32[2,4,256]{2,1,0:T(4,128)}, u32[]{:S(2)}) copy-start(f32[2,4,256]{2,1,0:T(4,128)} %get-tuple-element.8) | copy-start | bytes 24580

commit v4 on v3

--- a/solution.py
+++ b/solution.py
@@ -12,7 +12,7 @@
 HARM = 32
 RAD = 16
 NPHI = 768
-GROUP = 4
+GROUP = 8
 
 PAIRS = ((0, 3), (1, 2))
 EARLY = [(c, 0) for c in range(8)]
@@ -238,8 +238,8 @@
         landed = mode_part(modes, group, pl.ds(0, 256))
         pltpu.make_async_copy(landed, landed, mode_recv.at[group]).wait()
 
-    send_modes(0)
-    send_modes(1)
+    for group in range(3):
+        send_modes(group)
 
     order8 = me * 8 + iota((8, 128), 0)
     for half in range(2):
@@ -352,7 +352,6 @@
         jnp.where(((lane >> 4) & 1) == 0, early_c, early_s) * (mode_weight * mixed)
     ).astype(BF16)
     send_spectra(0)
-    send_modes(2)
     send_modes(3)
 
     def later(k):
@@ -552,17 +551,30 @@
     pltpu.make_async_copy(efin.at[pl.ds(0, 15)], efin.at[pl.ds(0, 15)], e_send.at[1]).wait()
 
 
+def hand_out(adv, grad, energy, adv_out, grad_out, energy_out, sem):
+    copies = [
+        pltpu.make_async_copy(source, target, sem.at[i])
+        for i, (source, target) in enumerate(
+            ((adv, adv_out), (grad, grad_out), (energy, energy_out))
+        )
+    ]
+    for copy in copies:
+        copy.start()
+    for copy in copies:
+        copy.wait()
+
+
 def local(velocity, magnetic, vorticity, current):
     vmem = pl.BlockSpec(memory_space=pltpu.VMEM)
     block = velocity.shape
-    return pl.pallas_call(
+    made = pl.pallas_call(
         kernel,
         out_shape=(
             jax.ShapeDtypeStruct(block, BF16),
             jax.ShapeDtypeStruct(block, BF16),
             jax.ShapeDtypeStruct((2, 4, L), F32),
         ),
-        in_specs=[pl.BlockSpec(memory_space=pl.ANY)] * 4,
+        in_specs=[pl.BlockSpec(memory_space=pltpu.HBM)] * 4,
         out_specs=(vmem,) * 3,
         scratch_shapes=[
             pltpu.VMEM((4,) + block, BF16),
@@ -602,8 +614,18 @@
             pltpu.SemaphoreType.DMA((2,)),
             pltpu.SemaphoreType.DMA((2,)),
         ],
-        compiler_params=pltpu.CompilerParams(collective_id=0, has_side_effects=True),
-    )(velocity, magnetic, vorticity, current)
+        compiler_params=pltpu.CompilerParams(
+            collective_id=0, has_side_effects=True, vmem_limit_bytes=40 * 1024 * 1024
+        ),
+    )(*(pltpu.with_memory_space_constraint(v, pltpu.HBM) for v in (velocity, magnetic, vorticity, current)))
+    return pl.pallas_call(
+        hand_out,
+        out_shape=tuple(jax.ShapeDtypeStruct(v.shape, v.dtype) for v in made),
+        in_specs=[pl.BlockSpec(memory_space=pl.ANY)] * 3,
+        out_specs=(pl.BlockSpec(memory_space=pltpu.HBM),) * 3,
+        scratch_shapes=[pltpu.SemaphoreType.DMA((3,))],
+        compiler_params=pltpu.CompilerParams(vmem_limit_bytes=1024 * 1024),
+    )(*made)
 
 
 def solution(mesh):

time: 47.2 us -> 43.2 us (0.915)
  the two profiles are of different devices: /device:TPU:7 before, /device:TPU:1 now
where the time goes in v4:
time: 43.2 us; the launch traced here: 43.1 us
  Pallas kernels  42.5 us (98%)
  between operations  0.64 us (1%)
    pallas_call x1, Pallas kernels, local(): pl.pallas_call(kernel, out_shape=(jax.ShapeDtypeStruct(block, BF16), jax....  41.7 us

profile of v4, /device:TPU:1, one launch (start us, length us, event | category | flops | bytes accessed | tf_op | source)
XLA Modules:
  0.0 43.1 jit_solution(4947006198454754086)
XLA Ops:
  0.6 41.7 %shard_map.67 = (bf16[3,4,2,8,256]{4,3,2,1,0:T(8,128)(2,1)S(1)}, bf16[3,4,2,8,256]{4,3,2,1,0:T(8,128)(2,1)S(1)}, f32[2,4,256]{2,1,0:T(4,128)S(1)}) custom-call(bf16[3,4,2,8,256]{4,3,2,1,0:T(8,128)(2,1)} %vel.1, bf16[3,4,2,8,256]{4,3,2,1,0:T(8,128)(2,1)} %mag.1, bf16[3,4,2,8,256]{4,3,2,1,0:T(8,128)(2,1)} %vor.1, bf16[3,4,2,8,256]{4,3,2,1,0:T(8,128)(2,1)} %cur.1), custom_call_target="tpu_custom_call" | custom-call | tf_op jit(solution)/shard_map/pallas_call | solution.py:570
  42.4 0.7 %shard_map.68 = (bf16[3,4,2,8,256]{4,3,2,1,0:T(8,128)(2,1)}, bf16[3,4,2,8,256]{4,3,2,1,0:T(8,128)(2,1)}, f32[2,4,256]{2,1,0:T(4,128)}) custom-call(bf16[3,4,2,8,256]{4,3,2,1,0:T(8,128)(2,1)S(1)} %get-tuple-element.6.adv, bf16[3,4,2,8,256]{4,3,2,1,0:T(8,128)(2,1)S(1)} %get-tuple-element.7.grad, f32[2,4,256]{2,1,0:T(4,128)S(1)} %get-tuple-element.8.energy), custom_call_target="tpu_custom_call" | custom-call | tf_op jit(solution)/shard_map/pallas_call | solution.py:621

commit v5 on v4

--- a/solution.py
+++ b/solution.py
@@ -12,7 +12,6 @@
 HARM = 32
 RAD = 16
 NPHI = 768
-GROUP = 8
 
 PAIRS = ((0, 3), (1, 2))
 EARLY = [(c, 0) for c in range(8)]
@@ -134,10 +133,6 @@
     def _():
         pl.semaphore_signal(barrier, inc=1, device_id={"rad": my_rad + 1})
 
-    @pl.when(below)
-    def _():
-        pl.semaphore_signal(barrier, inc=1, device_id={"rad": my_rad - 1})
-
     arrivals = [
         pltpu.make_async_copy(ref, fields.at[a], field_sem.at[a])
         for a, ref in enumerate((vel, mag, vor, cur))
@@ -155,30 +150,30 @@
 
     legendre_steps(me, tab)
 
-    for a, arrival in enumerate(arrivals):
+    def spread(c, pair):
+        for r in range(2):
+            both = [fields[c // 3, c % 3, shell, r].astype(F32) for shell in PAIRS[pair]]
+            both = jnp.concatenate(both, axis=0)
+            at = ((r * 12 + c) * 2 + pair) * 64
+            for half in range(2):
+                part = both[:, half * 128:(half + 1) * 128]
+                for copy in range(4):
+                    coef[half, at + copy * 16:at + copy * 16 + 16, :] = part
+
+    for arrival in arrivals:
         arrival.wait()
-        for c in range(3):
-            for r in range(2):
-                for pair in range(2):
-                    both = fields[a, c, PAIRS[pair][0], r], fields[a, c, PAIRS[pair][1], r]
-                    both = jnp.concatenate([v.astype(F32) for v in both], axis=0)
-                    at = ((r * 12 + a * 3 + c) * 2 + pair) * 64
-                    for half in range(2):
-                        part = both[:, half * 128:(half + 1) * 128]
-                        for copy in range(4):
-                            coef[half, at + copy * 16:at + copy * 16 + 16, :] = part
+    for c, pair in EARLY:
+        spread(c, pair)
 
     slot_row = iota((8, 128), 0)
 
-    def synthesis(m, slot):
-        for jt, rows in ((0, 128), (1, 64)):
-            table = tab[jt, pl.ds(m, L, stride=8), :]
-            qt[m, jt * 128:jt * 128 + rows, :] = table.T[0:rows].astype(BF16)
+    def synthesis(m, tiles):
+        first_row, last_row = tiles[0] * 128, tiles[-1] * 128 + 128
         sign = parity_sign(m, 8)
         for half in range(2):
             sgn = jnp.where(slot_row >= 4, sign[:, half * 128:(half + 1) * 128], 1.0)
             keep = [jnp.where(((slot_row >> 1) & 1) == gn, sgn, 0.0) for gn in range(2)]
-            for row in range(0, 384, 16):
+            for row in range(first_row, last_row, 16):
                 values = []
                 for at in (row, row + 8):
                     c, pair, r = ROW_SLOT[at]
@@ -186,26 +181,26 @@
                     values.append(coef[half, pl.ds(first + m, 8, stride=8), :])
                 for gn in range(2):
                     lane = gn * 256 + half * 128
-                    rhs[slot, row:row + 16, lane:lane + 128] = jnp.concatenate(
+                    rhs[m, row:row + 16, lane:lane + 128] = jnp.concatenate(
                         [v * keep[gn] for v in values], axis=0
                     ).astype(BF16)
         lhs = jnp.concatenate([qt[m, 0:96, :], qt[m, 96:192, :]], axis=1)
-        made = dot_nt(lhs, rhs[slot]) * (1.0 / L)
+        made = dot_nt(lhs, rhs[m, first_row:last_row]) * (1.0 / L)
         for k in range(3):
-            for lt in range(3):
+            for lt in tiles:
+                lane = lt * 128 - first_row
                 synth[k, lt, pl.ds(m, 32, stride=8), :] = made[
-                    k * 32:(k + 1) * 32, lt * 128:(lt + 1) * 128
+                    k * 32:(k + 1) * 32, lane:lane + 128
                 ]
 
-    def synthesis_group(group, carry):
-        for inner in range(GROUP):
-            synthesis(group * GROUP + inner, inner)
-        return carry
-
-    lax.fori_loop(0, 8 // GROUP, synthesis_group, 0)
-    wire[...] = synth[...].astype(BF16)
-
-    pl.semaphore_wait(barrier, HARM - 1 + above.astype(jnp.int32) + below.astype(jnp.int32))
+    for m in range(8):
+        for jt, rows in ((0, 128), (1, 64)):
+            table_of = tab[jt, pl.ds(m, L, stride=8), :]
+            qt[m, jt * 128:jt * 128 + rows, :] = table_of.T[0:rows].astype(BF16)
+        synthesis(m, (0,))
+    wire[:, 0] = synth[:, 0].astype(BF16)
+
+    pl.semaphore_wait(barrier, HARM - 1 + below.astype(jnp.int32))
 
     def rows_of(device):
         return pl.ds(pl.multiple_of(device * 8, 8), 8)
@@ -238,8 +233,15 @@
         landed = mode_part(modes, group, pl.ds(0, 256))
         pltpu.make_async_copy(landed, landed, mode_recv.at[group]).wait()
 
-    for group in range(3):
-        send_modes(group)
+    send_modes(0)
+
+    for c, pair in LATER:
+        spread(c, pair)
+    for m in range(8):
+        synthesis(m, (1, 2))
+    wire[:, 1:3] = synth[:, 1:3].astype(BF16)
+    send_modes(1)
+    send_modes(2)
 
     order8 = me * 8 + iota((8, 128), 0)
     for half in range(2):
@@ -501,6 +503,7 @@
 
     @pl.when(above)
     def _():
+        halo_down().wait_recv()
         halo_up().start()
 
     keep_induction(1)
@@ -536,7 +539,6 @@
     @pl.when(above)
     def _():
         halo_up().wait_send()
-        halo_down().wait_recv()
 
     grad[:, 3] = ((high[...].astype(F32) - shells[2]) * 0.5).astype(BF16)
 
@@ -581,7 +583,7 @@
             pltpu.VMEM((2, L * 8, 128), F32),
             pltpu.VMEM((8, 192, L), BF16),
             pltpu.VMEM((2, 48 * 64, 128), F32),
-            pltpu.VMEM((GROUP, 384, 512), BF16),
+            pltpu.VMEM((8, 384, 512), BF16),
             pltpu.VMEM((3, 3, 256, 128), F32),
             pltpu.VMEM((3, 3, 256, 128), BF16),
             pltpu.VMEM((3, 3, 256, 128), BF16),

time: 43.2 us -> 43.4 us (level)
  no operation moved by 1% of the time
where the time goes in v5:
time: 43.4 us; the launch traced here: 43.2 us
  Pallas kernels  42.6 us (98%)
  between operations  0.64 us (1%)
    pallas_call x1, Pallas kernels, local(): pl.pallas_call(kernel, out_shape=(jax.ShapeDtypeStruct(block, BF16), jax....  41.9 us

profile of v5, /device:TPU:1, one launch (start us, length us, event | category | flops | bytes accessed | tf_op | source)
XLA Modules:
  0.0 43.2 jit_solution(271828005792924930)
XLA Ops:
  0.6 41.9 %shard_map.67 = (bf16[3,4,2,8,256]{4,3,2,1,0:T(8,128)(2,1)S(1)}, bf16[3,4,2,8,256]{4,3,2,1,0:T(8,128)(2,1)S(1)}, f32[2,4,256]{2,1,0:T(4,128)S(1)}) custom-call(bf16[3,4,2,8,256]{4,3,2,1,0:T(8,128)(2,1)} %vel.1, bf16[3,4,2,8,256]{4,3,2,1,0:T(8,128)(2,1)} %mag.1, bf16[3,4,2,8,256]{4,3,2,1,0:T(8,128)(2,1)} %vor.1, bf16[3,4,2,8,256]{4,3,2,1,0:T(8,128)(2,1)} %cur.1), custom_call_target="tpu_custom_call" | custom-call | tf_op jit(solution)/shard_map/pallas_call | solution.py:572
  42.5 0.7 %shard_map.68 = (bf16[3,4,2,8,256]{4,3,2,1,0:T(8,128)(2,1)}, bf16[3,4,2,8,256]{4,3,2,1,0:T(8,128)(2,1)}, f32[2,4,256]{2,1,0:T(4,128)}) custom-call(bf16[3,4,2,8,256]{4,3,2,1,0:T(8,128)(2,1)S(1)} %get-tuple-element.6.adv, bf16[3,4,2,8,256]{4,3,2,1,0:T(8,128)(2,1)S(1)} %get-tuple-element.7.grad, f32[2,4,256]{2,1,0:T(4,128)S(1)} %get-tuple-element.8.energy), custom_call_target="tpu_custom_call" | custom-call | tf_op jit(solution)/shard_map/pallas_call | solution.py:623
